TPU v7x, 256 devices: a whole 4x4x8 slice. The times are simulated.
256 devices in a mesh: gx: 8 (over z), gy: 4 (over y), gz: 8 (over x, core).
Axes of the slice: x: 4, y: 4, z: 8, core: 2. Of those that a mesh axis runs over, the one named last changes fastest.
Arguments:
- source_points: float32 [3, 13, 8, 16, 16, 512], P(None, None, 'gx', 'gy', 'gz'), may hold values from -3 to 3
- target_points: float32 [3, 13, 8, 16, 16, 512], P(None, None, 'gx', 'gy', 'gz'), may hold values from -3 to 3
- normals: float32 [3, 13, 8, 16, 16, 512], P(None, None, 'gx', 'gy', 'gz'), may hold values from -4 to 4
- weights: float32 [13, 8, 16, 16, 512], P(None, 'gx', 'gy', 'gz'), may hold values from 0.1 to 1
- blocks: int32 [13, 8, 16, 16], P(None, 'gx', 'gy', 'gz'), may hold values from 0 to 2
- affines: float32 [12, 8, 16, 16], P(None, 'gx', 'gy', 'gz'), may hold values from -0.5 to 0.5
- anchor: int32 [1], replicated, may hold values from 0 to 2047
Outputs:
- update: float32 [12, 8, 16, 16], P(None, 'gx', 'gy', 'gz')
- residual: float32 [12, 8, 16, 16], P(None, 'gx', 'gy', 'gz')
Inputs may be any that keep to these rules, and one draw needn't show every extreme that they name: `blocks`: number of 256-point correspondence blocks of the correlation; entries of correlations whose second tile lies outside the grid are not read. `anchor`: a tile index (x 16 + y) * 16 + z.
All inputs are finite; a program needn't handle non-finite values.
Results may differ from a plain program's by a relative error of at most 0.0003.
Values sent between devices are 32-bit elements; how exact they have to be, the bound alone decides.
A program may use at most 128 MiB of HBM per device.

v0:
```python
import functools

import jax
import jax.numpy as jnp
from jax import lax
from jax.experimental import pallas as pl
from jax.experimental.pallas import tpu as pltpu
from jax.sharding import PartitionSpec as P

BLOCK = 256
ITERS = 10
STEP = 2
SPACING = 0.5
DAMPING = 1.0
OFFSETS = (
    (1, 0, 0),
    (0, 1, 0),
    (0, 0, 1),
    (1, 1, -1),
    (1, -1, 1),
    (-1, 1, 1),
    (1, 1, 0),
    (1, 0, 1),
    (0, 1, 1),
    (1, 1, 1),
    (1, -1, 0),
    (0, 1, -1),
    (-1, 0, 1),
)
AXES = ("gx", "gy", "gz")
MESH = pl.DeviceIdType.MESH
LANES = 128
TY, TZ, TILES = 4, 2, 8
COMPS = 12
ROWS = COMPS * TILES
WIDE = ROWS + TILES
F32 = jnp.float32


def shifts(offset):
    seconds = (0,) if offset[1] == 0 else (0, offset[1])
    thirds = (0,) if offset[2] == 0 else (0, offset[2])
    return [(offset[0], y, z) for y in seconds for z in thirds]


SELF = (0, 0, 0)
REACH = (SELF, *sorted({s for o in OFFSETS for s in shifts(o)} - {SELF}))
OTHERS = len(REACH) - 1
GREET = tuple(sorted({s for s in REACH[1:]} | {tuple(-p for p in s) for s in REACH[1:]}))


def pieces():
    found = []
    for index, offset in enumerate(OFFSETS):
        for shift in shifts(offset):
            if shift == SELF:
                continue
            if offset[1] == 0:
                low, count = 0, TY
            elif shift[1] == 0:
                low, count = (1 if offset[1] > 0 else 0), TY - 1
            else:
                low, count = (0 if offset[1] > 0 else TY - 1), 1
            found.append((index, shift, low, count, 0 if shift[2] == 0 else 1))
    return tuple(found)


PIECES = pieces()


def device_at(shift, sign):
    there = []
    for axis, part in zip(AXES, shift):
        size = lax.axis_size(axis)
        there.append(lax.rem(lax.axis_index(axis) + (sign * part + size), size))
    return tuple(there)


def remote(source, target, sent, got, device):
    return pltpu.make_async_remote_copy(
        src_ref=source,
        dst_ref=target,
        send_sem=sent,
        recv_sem=got,
        device_id=device,
        device_id_type=MESH,
    )


def exchange_kernel(target, affine, near, far, affine_there, sent, got):
    barrier = pltpu.get_barrier_semaphore()
    for shift in GREET:
        pl.semaphore_signal(barrier, inc=1, device_id=device_at(shift, 1), device_id_type=MESH)
    pl.semaphore_wait(barrier, len(GREET))
    copies = []
    for number, (index, shift, low, count, which) in enumerate(PIECES):
        span = pl.ds(low, count)
        place = (near, far)[which]
        copies.append(
            remote(
                target.at[:, index, 0, span],
                place.at[:, index, span],
                sent.at[number],
                got.at[number],
                device_at(shift, -1),
            )
        )
    for number, shift in enumerate(REACH[1:]):
        at = len(PIECES) + number
        copies.append(
            remote(affine, affine_there.at[number], sent.at[at], got.at[at], device_at(shift, -1))
        )
    for copy in copies:
        copy.start()
    for copy in copies:
        copy.wait()


def iotas(rows=TILES):
    return (
        lax.broadcasted_iota(jnp.int32, (rows, LANES), 0),
        lax.broadcasted_iota(jnp.int32, (rows, LANES), 1),
    )


def tiled(mask, times):
    return jnp.concatenate([mask] * times, axis=0)


def cross(left, right):
    return lax.dot_general(
        left,
        right,
        (((1,), (1,)), ((), ())),
        precision=lax.Precision.HIGHEST,
        preferred_element_type=F32,
    )


def moments_kernel(
    source,
    target,
    near,
    far,
    normal,
    weight,
    affine,
    blocks,
    shares,
    own,
    slab,
    here,
    here_weighted,
    there,
    there_weighted,
    packed,
):
    sub, lane = iotas()
    slot = lane & (TILES - 1)
    blocks[...] = jnp.zeros_like(blocks)
    shares[...] = jnp.zeros_like(shares)
    own[...] = jnp.zeros_like(own)
    packed[...] = jnp.zeros_like(packed)
    here[WIDE:, :] = jnp.zeros((LANES - WIDE, here.shape[1]), F32)
    there[ROWS:, :] = jnp.zeros((LANES - ROWS, there.shape[1]), F32)
    same = sub == slot
    for index, offset in enumerate(OFFSETS):
        for y in range(TY):
            for c in range(3):
                slab[c, 2 * y : 2 * y + 2, :] = source[c, index, 0, y]
                slab[3 + c, 2 * y : 2 * y + 2, :] = normal[c, index, 0, y]
        for y in range(TY):
            before = (y - offset[1]) % TY
            shift_y = (y - offset[1]) // TY
            for z in range(TZ):
                back = (z - offset[2]) % TZ
                shift_z = (z - offset[2]) // TZ
                shift = (offset[0], -shift_y, -shift_z)
                to, come = y * TZ + z, before * TZ + back
                for c in range(3):
                    slab[6 + c, to : to + 1, :] = normal[c, index, 0, before, back : back + 1, :]
                    if shift == SELF:
                        row = target[c, index, 0, y, z : z + 1, :]
                    elif shift[2] == 0:
                        row = near[c, index, y, z : z + 1, :]
                    else:
                        row = far[c, index, y, z : z + 1, :]
                    slab[9 + c, to : to + 1, :] = row
                slab[12, to : to + 1, :] = weight[index, come : come + 1, :]
        share, share_there = weight[index], slab[12]
        for c in range(3):
            n, m = slab[3 + c], slab[6 + c]
            for e in range(4):
                at = (4 * c + e) * TILES
                a = n * slab[e] if e < 3 else n
                b = -(m * slab[9 + e]) if e < 3 else -m
                here[at : at + TILES, :] = a
                here_weighted[at : at + TILES, :] = a * share
                there[at : at + TILES, :] = b
                there_weighted[at : at + TILES, :] = b * share_there
        along = sum(part * slab[3 + c] for c, part in enumerate(offset) if part != 0)
        here[ROWS:WIDE, :] = along
        here_weighted[ROWS:WIDE, :] = along * share
        own[...] += cross(here_weighted[:ROWS, :], here[...])
        pair = cross(here_weighted[...], there[...])
        back = cross(there_weighted[...], there[...])
        for a in range(COMPS):
            at = a * TILES
            packed[a : a + 1, :] = jnp.sum(
                jnp.where(same, back[at : at + TILES, :], 0.0), axis=0, keepdims=True
            )
        second, third = sub // TZ + offset[1], sub % TZ + offset[2]
        slot_y, slot_z = slot // TZ, slot % TZ
        all_slots = packed[...]
        for shift in shifts(offset):
            j = REACH.index(shift)
            meets = (slot_y + TY * shift[1] == second) & (slot_z + TZ * shift[2] == third)
            blocks[j] += jnp.where(tiled(meets, WIDE // TILES), pair, 0.0)
            owned = jnp.ones((TILES, LANES), jnp.bool_)
            from_y, from_z = slot_y - offset[1] + TY * shift[1], slot_z - offset[2] + TZ * shift[2]
            owned = (from_y >= 0) & (from_y < TY) & (from_z >= 0) & (from_z < TZ)
            shares[j] += jnp.where(tiled(owned, 2), all_slots, 0.0)
    own[...] = jnp.where(tiled(same, COMPS), own[...], 0.0)
    row = affine[0]
    columns = [
        jnp.sum(jnp.where(lane == sub + a * TILES, row, 0.0), axis=1, keepdims=True)
        for a in range(COMPS + 1)
    ]
    for j in range(OTHERS + 1):
        total = jnp.zeros((TILES, LANES), F32)
        for a in range(COMPS + 1):
            total = total + blocks[j, a * TILES : (a + 1) * TILES, :] * columns[a]
        shares[j, COMPS : COMPS + 1, :] = jnp.sum(total, axis=0, keepdims=True)


def solve_kernel(steps, groups, *refs):
    blocks, shares, own, affine, affine_there, keep = refs[:6]
    update, residual = refs[6:8]
    shares_there, matrix, inverse, plane, basis, lifted_basis = refs[8:14]
    pair_sum, line_sum, pair_send, line_send = refs[14:18]
    rest = refs[18:]
    send_rows, got_rows, back_rows, got_back = (rest[k * steps : (k + 1) * steps] for k in range(4))
    share_sent, share_got, halo_sems, sum_sems = rest[4 * steps :]
    count = 2 * steps + 1
    first, second, third = (lax.axis_index(a) for a in AXES)
    size_first, size_second, size_third = (lax.axis_size(a) for a in AXES)
    in_pair = second * size_third + third
    pair_size = size_second * size_third

    def pair_peer(k):
        there = lax.rem(in_pair + k, pair_size)
        return (first, there // size_third, lax.rem(there, size_third))

    def line_peer(k):
        return (lax.rem(first + k, size_first), second, third)

    barrier = pltpu.get_barrier_semaphore()
    for shift in GREET:
        pl.semaphore_signal(barrier, inc=1, device_id=device_at(shift, 1), device_id_type=MESH)

    @pl.loop(1, pair_size)
    def _(k):
        pl.semaphore_signal(barrier, inc=1, device_id=pair_peer(k), device_id_type=MESH)

    @pl.loop(1, size_first)
    def _(k):
        pl.semaphore_signal(barrier, inc=1, device_id=line_peer(k), device_id_type=MESH)

    pl.semaphore_wait(barrier, len(GREET) + pair_size - 1 + size_first - 1)

    for number, shift in enumerate(REACH[1:]):
        remote(
            shares.at[number + 1],
            shares_there.at[number],
            share_sent,
            share_got,
            device_at(shift, 1),
        ).start()

    sub, lane = iotas()
    slot = lane & (TILES - 1)
    same = sub == slot
    eyes = [lane == sub + a * TILES for a in range(COMPS)]
    wide_sub, wide_lane = iotas(16)

    def column(row):
        return [jnp.sum(jnp.where(eyes[a], row, 0.0), axis=1, keepdims=True) for a in range(COMPS)]

    def group(a):
        return slice(a * TILES, (a + 1) * TILES)

    keep_row = keep[0]
    keep_column = column(keep_row)
    row = affine[0]
    sums = []
    for a in range(COMPS):
        total = own[group(a), :] * row + blocks[0, group(a), :] * row
        for j in range(OTHERS):
            total = total + blocks[j + 1, group(a), :] * affine_there[j]
        sums.append(total)
    everything = pltpu.make_async_copy(shares_there, shares_there, share_got)
    everything.wait()
    pltpu.make_async_copy(shares_there, shares_there, share_sent).wait()
    gathered = shares[0]
    for j in range(OTHERS):
        gathered = gathered + shares_there[j]
    right = []
    for a in range(COMPS):
        spread = jnp.where(same & (lane < ROWS), gathered[a : a + 1, :], 0.0)
        total = sums[a] + spread * row + jnp.where(eyes[a], gathered[COMPS : COMPS + 1, :], 0.0)
        right.append(-keep_column[a] * jnp.sum(total, axis=1, keepdims=True))
        mine = jnp.where(lane < ROWS, own[group(a), :], 0.0)
        compact = jnp.sum(mine, axis=0, keepdims=True) + gathered[a : a + 1, :]
        unit = jnp.where((lane[:1] >= a * TILES) & (lane[:1] < (a + 1) * TILES), 1.0, 0.0)
        compact = keep_row * (compact + DAMPING * unit) + (1.0 - keep_row) * unit
        picked = jnp.where(wide_lane // TILES == wide_sub, compact, 0.0)
        for by in (8, 16, 32, 64):
            picked = picked + pltpu.roll(picked, by, 1)
        matrix[a] = picked

    rows = [matrix[a] for a in range(COMPS)]
    for k in range(COMPS):
        factor = 1.0 / rows[k][k : k + 1, :]
        at_pivot = wide_sub == k
        pivot_row = jnp.where(at_pivot, factor, rows[k] * factor)
        for i in range(COMPS):
            if i != k:
                f = rows[i][k : k + 1, :]
                rows[i] = jnp.where(at_pivot, 0.0, rows[i]) - f * pivot_row
        rows[k] = pivot_row
    for a in range(COMPS):
        compact = jnp.sum(
            jnp.where(wide_lane // TILES == wide_sub, rows[a], 0.0), axis=0, keepdims=True
        )
        inverse[group(a), :] = jnp.where(same & (lane < ROWS), compact, 0.0)

    def as_row(col):
        total = jnp.zeros((TILES, LANES), F32)
        for a in range(COMPS):
            total = total + jnp.where(eyes[a], col[a], 0.0)
        return jnp.sum(total, axis=0, keepdims=True)

    def precondition(col):
        total = jnp.zeros((TILES, LANES), F32)
        for a in range(COMPS):
            total = total + inverse[group(a), :] * col[a]
        return jnp.sum(total, axis=0, keepdims=True)

    def couple(step, vectors):
        amount = len(vectors)
        cols = [column(v) for v in vectors]
        for r, v in enumerate(vectors):
            send_rows[step][0, r : r + 1, :] = v
        for number, shift in enumerate(REACH[1:]):
            remote(
                send_rows[step].at[0],
                got_rows[step].at[number],
                halo_sems.at[step, 0],
                halo_sems.at[step, 1],
                device_at(shift, -1),
            ).start()
        local = []
        for j in range(OTHERS + 1):
            totals = [jnp.zeros((TILES, LANES), F32) for _ in vectors]
            for a in range(COMPS):
                block = blocks[j, group(a), :]
                for r in range(amount):
                    totals[r] = totals[r] + block * cols[r][a]
            for r in range(amount):
                total = jnp.sum(totals[r], axis=0, keepdims=True)
                if j == 0:
                    local.append(total)
                else:
                    back_rows[step][j - 1, r : r + 1, :] = total
            if j > 0:
                remote(
                    back_rows[step].at[j - 1],
                    got_back[step].at[j - 1],
                    halo_sems.at[step, 2],
                    halo_sems.at[step, 3],
                    device_at(REACH[j], 1),
                ).start()
        sums = [[blocks[0, group(a), :] * v for a in range(COMPS)] for v in vectors]
        rows_there, back_there = got_rows[step], got_back[step]
        pltpu.make_async_copy(rows_there, rows_there, halo_sems.at[step, 1]).wait()
        for j in range(OTHERS):
            for r in range(amount):
                v = rows_there[j, r : r + 1, :]
                for a in range(COMPS):
                    sums[r][a] = sums[r][a] + blocks[j + 1, group(a), :] * v
        pltpu.make_async_copy(back_there, back_there, halo_sems.at[step, 3]).wait()
        results = []
        for r in range(amount):
            came = local[r]
            for j in range(OTHERS):
                came = came + back_there[j, r : r + 1, :]
            results.append(
                [
                    keep_column[a]
                    * jnp.sum(sums[r][a] + jnp.where(eyes[a], came, 0.0), axis=1, keepdims=True)
                    for a in range(COMPS)
                ]
            )
        pltpu.make_async_copy(rows_there, rows_there, halo_sems.at[step, 0]).wait()
        pltpu.make_async_copy(back_there, back_there, halo_sems.at[step, 2]).wait()
        return results

    def reduce_all(value, parity):
        pair_send[parity] = value
        pair_sum[parity, in_pair] = value

        @pl.loop(1, pair_size)
        def _(k):
            remote(
                pair_send.at[parity],
                pair_sum.at[parity, in_pair],
                sum_sems.at[parity, 0],
                sum_sems.at[parity, 1],
                pair_peer(k),
            ).start()

        part = pair_sum.at[parity, pl.ds(0, pair_size - 1)]
        pltpu.make_async_copy(part, part, sum_sems.at[parity, 1]).wait()
        total = pair_sum[parity, 0]
        for k in range(1, pair_size):
            total = total + pair_sum[parity, k]
        line_send[parity] = total
        line_sum[parity, first] = total

        @pl.loop(1, size_first)
        def _(k):
            remote(
                line_send.at[parity],
                line_sum.at[parity, first],
                sum_sems.at[parity, 2],
                sum_sems.at[parity, 3],
                line_peer(k),
            ).start()

        row_part = line_sum.at[parity, pl.ds(0, size_first - 1)]
        pltpu.make_async_copy(row_part, row_part, sum_sems.at[parity, 3]).wait()
        total = line_sum[parity, 0]
        for k in range(1, size_first):
            total = total + line_sum[parity, k]
        pltpu.make_async_copy(part, part, sum_sems.at[parity, 0]).wait()
        pltpu.make_async_copy(row_part, row_part, sum_sems.at[parity, 2]).wait()
        return total

    basis[...] = jnp.zeros_like(basis)
    lifted_basis[...] = jnp.zeros_like(lifted_basis)
    start, start_lifted = as_row(right), precondition(right)
    for at in (0, steps + 1):
        basis[at : at + 1, :] = start
        lifted_basis[at : at + 1, :] = start_lifted
    update[...] = jnp.zeros_like(update)

    major = jnp.zeros((TILES, LANES), jnp.int32)
    for k in range(1, count + 1):
        major = major + jnp.where(lane >= k * count, 1, 0)
    minor = lane - count * major

    def form(mask):
        return jnp.where(mask & (lane < count * count), 1.0, 0.0)

    @pl.loop(0, groups)
    def _(number):
        for step in range(steps):
            places = [step] + ([steps + 1 + step] if step < steps - 1 else [])
            found = couple(step, [lifted_basis[at : at + 1, :] for at in places])
            for at, col in zip(places, found):
                basis[at + 1 : at + 2, :] = as_row(col)
                lifted_basis[at + 1 : at + 2, :] = precondition(col)
        gram = cross(basis[...], lifted_basis[...])
        spread = jnp.zeros((16, LANES), F32)
        for k in range(count):
            moved = pltpu.roll(gram, k * count, 1) if k else gram
            spread = spread + jnp.where(wide_sub == k, moved, 0.0)
        mine = jnp.sum(spread, axis=0, keepdims=True)
        g = jnp.broadcast_to(reduce_all(mine, lax.rem(number, 2)), (TILES, LANES))

        def inner(x, y):
            return jnp.sum(g * x * y, axis=1, keepdims=True)

        p_major, p_minor = form(major == 0), form(minor == 0)
        r_major, r_minor = form(major == steps + 1), form(minor == steps + 1)
        u_minor = jnp.zeros((TILES, LANES), F32)
        product = inner(r_major, r_minor)
        for _ in range(steps):
            a_major = p_major + pltpu.roll(p_major, count, 1)
            a_minor = p_minor + pltpu.roll(p_minor, 1, 1)
            alpha = product / inner(p_major, a_minor)
            u_minor = u_minor + alpha * p_minor
            r_major = r_major - alpha * a_major
            r_minor = r_minor - alpha * a_minor
            following = inner(r_major, r_minor)
            ratio = following / product
            p_major = r_major + ratio * p_major
            p_minor = r_minor + ratio * p_minor
            product = following

        def combined(minor_form, vectors):
            both = jnp.concatenate([minor_form, minor_form], axis=0)
            weights = jnp.sum(
                jnp.where((wide_lane == wide_sub) & (wide_lane < count), both, 0.0),
                axis=1,
                keepdims=True,
            )
            return jnp.sum(weights * vectors, axis=0, keepdims=True)

        ys, zs = basis[...], lifted_basis[0:16, :]
        update[...] += combined(u_minor, zs)
        for at, shape in ((0, p_minor), (steps + 1, r_minor)):
            basis[at : at + 1, :] = combined(shape, ys)
            lifted_basis[at : at + 1, :] = combined(shape, zs)

    residual[...] = basis[steps + 1 : steps + 2, :]


def vmem(*shape):
    return pltpu.VMEM(shape, F32)


def on_device(source_points, target_points, normals, weights, blocks, affines, anchor):
    points = source_points.shape[5]
    dirs = len(OFFSETS)
    in_vmem = pl.BlockSpec(memory_space=pltpu.VMEM)
    sizes = [lax.axis_size(a) for a in AXES]

    tile = jnp.arange(TILES, dtype=jnp.int32)
    x = lax.axis_index("gx")
    y = lax.axis_index("gy") * TY + tile // TZ
    z = lax.axis_index("gz") * TZ + tile % TZ
    spans = (sizes[0], sizes[1] * TY, sizes[2] * TZ)
    keep = ((x * spans[1] + y) * spans[2] + z != anchor[0]).astype(F32)
    keep_row = jnp.pad(jnp.tile(keep, COMPS), (0, LANES - ROWS)).reshape(1, 1, LANES)
    identity = jnp.eye(3, 4, dtype=F32).reshape(COMPS, 1)
    matrix = (affines.reshape(COMPS, TILES) + identity).reshape(-1)
    affine_row = jnp.concatenate(
        [matrix, jnp.full((TILES,), -SPACING, F32), jnp.zeros((LANES - WIDE,), F32)]
    ).reshape(1, 1, LANES)
    offsets = jnp.array(OFFSETS, jnp.int32).T[:, :, None]
    there = [p + o for p, o in zip((x, y, z), offsets)]
    inside = functools.reduce(
        jnp.logical_and, [(p >= 0) & (p < span) for p, span in zip(there, spans)]
    )
    limit = jnp.where(inside, BLOCK * blocks.reshape(dirs, TILES), 0)
    slots = jnp.arange(points, dtype=jnp.int32)
    live = (slots < limit[..., None]).astype(F32)
    weight = weights.reshape(dirs, TILES, points) * live

    moved = jax.ShapeDtypeStruct((3, dirs, TY, TZ, points), F32)
    copies = len(PIECES) + OTHERS
    near, far, affine_there = pl.pallas_call(
        exchange_kernel,
        out_shape=(moved, moved, jax.ShapeDtypeStruct((OTHERS, 1, LANES), F32)),
        in_specs=[in_vmem] * 2,
        out_specs=[in_vmem] * 3,
        scratch_shapes=[pltpu.SemaphoreType.DMA((copies,)), pltpu.SemaphoreType.DMA((copies,))],
        compiler_params=pltpu.CompilerParams(
            collective_id=0, has_side_effects=True, vmem_limit_bytes=60 * 2**20
        ),
        name="exchange",
    )(target_points, affine_row[0])

    pairs, shares, own = pl.pallas_call(
        moments_kernel,
        out_shape=(
            jax.ShapeDtypeStruct((OTHERS + 1, WIDE, LANES), F32),
            jax.ShapeDtypeStruct((OTHERS + 1, 16, LANES), F32),
            jax.ShapeDtypeStruct((ROWS, LANES), F32),
        ),
        in_specs=[in_vmem] * 7,
        out_specs=[in_vmem] * 3,
        scratch_shapes=[
            vmem(13, TILES, points),
            vmem(LANES, points),
            vmem(WIDE, points),
            vmem(LANES, points),
            vmem(ROWS, points),
            vmem(16, LANES),
        ],
        compiler_params=pltpu.CompilerParams(vmem_limit_bytes=60 * 2**20),
        name="moments",
    )(source_points, target_points, near, far, normals, weight, affine_row)

    steps = STEP
    amounts = [2] * (steps - 1) + [1]
    pair_size = sizes[1] * sizes[2]
    update, residual = pl.pallas_call(
        functools.partial(solve_kernel, steps, ITERS // steps),
        out_shape=(jax.ShapeDtypeStruct((1, LANES), F32),) * 2,
        in_specs=[in_vmem] * 6,
        out_specs=[in_vmem] * 2,
        scratch_shapes=[
            vmem(OTHERS, 16, LANES),
            vmem(COMPS, 16, LANES),
            vmem(ROWS, LANES),
            vmem(16, LANES),
            vmem(16, LANES),
            vmem(LANES, LANES),
            vmem(2, pair_size, 1, LANES),
            vmem(2, sizes[0], 1, LANES),
            vmem(2, 1, LANES),
            vmem(2, 1, LANES),
            *[vmem(1, r, LANES) for r in amounts],
            *[vmem(OTHERS, r, LANES) for r in amounts],
            *[vmem(OTHERS, r, LANES) for r in amounts],
            *[vmem(OTHERS, r, LANES) for r in amounts],
            pltpu.SemaphoreType.DMA,
            pltpu.SemaphoreType.DMA,
            pltpu.SemaphoreType.DMA((steps, 4)),
            pltpu.SemaphoreType.DMA((2, 4)),
        ],
        compiler_params=pltpu.CompilerParams(
            collective_id=1, has_side_effects=True, vmem_limit_bytes=60 * 2**20
        ),
        name="solve",
    )(pairs, shares, own, affine_row, affine_there, keep_row)
    shape = affines.shape
    return update[0, :ROWS].reshape(shape), residual[0, :ROWS].reshape(shape)


def solution(mesh):
    placed = (
        P(None, None, "gx", "gy", "gz", None),
        P(None, None, "gx", "gy", "gz", None),
        P(None, None, "gx", "gy", "gz", None),
        P(None, "gx", "gy", "gz", None),
        P(None, "gx", "gy", "gz"),
        P(None, "gx", "gy", "gz"),
        P(),
    )
    return jax.shard_map(
        on_device,
        mesh=mesh,
        in_specs=placed,
        out_specs=(P(None, "gx", "gy", "gz"), P(None, "gx", "gy", "gz")),
        check_vma=False,
    )
```

profile of v0, /device:TPU:1, one launch (start us, length us, event | category | flops | bytes accessed | tf_op | source)
XLA Modules:
  0.0 158.2 jit_solution(15829920974948749681)
XLA Ops:
  1.3 0.0 copy-start.6
  1.3 0.0 copy-start.1
  1.4 0.6 copy-done.6
  2.0 0.1 reshape.192
  2.1 0.0 copy-done.1
  2.1 0.0 copy-start.4
  2.1 0.0 copy-start.5
  2.1 0.6 copy-done.4
  2.7 0.0 copy-done.5
  2.7 0.1 fusion.4
  2.8 0.1 copy.15
  2.9 0.1 add.127
  3.0 0.1 add.128
  3.1 0.0 copy-start
  3.1 0.1 tile.10
  3.2 0.6 pad_bitcast_fusion.refs_5_
  3.8 0.0 copy-done
  3.8 0.1 copy.14
  3.9 0.1 reshape.188
  4.0 0.6 fusion.9
  4.6 1.1 reshape.189
  5.7 0.8 fusion.weight
  6.5 24.4 %exchange.1 = (f32[3,13,4,2,512]{4,3,2,1,0:T(2,128)}, f32[3,13,4,2,512]{4,3,2,1,0:T(2,128)}, f32[17,1,128]{2,1,0:T(1,128)}) custom-call(f32[3,13,1,4,2,512]{5,4,3,2,1,0:T(2,128)} %target.3, f32[1,128]{1,0:T(1,128)} %get-tuple-element.23.affine), custom_call_target="tpu_custom_call" | custom-call | tf_op jit(solution)/shard_map/exchange/pallas_call | solution.py:553
  30.8 9.8 %moments.1 = (f32[18,104,128]{2,1,0:T(8,128)}, f32[18,16,128]{2,1,0:T(8,128)}, f32[96,128]{1,0:T(8,128)}) custom-call(f32[3,13,1,4,2,512]{5,4,3,2,1,0:T(2,128)} %source.1, f32[3,13,1,4,2,512]{5,4,3,2,1,0:T(2,128)} %target.3, f32[3,13,4,2,512]{4,3,2,1,0:T(2,128)} %get-tuple-element.10.near, f32[3,13,4,2,512]{4,3,2,1,0:T(2,128)} %get-tuple-element.11.far, ...), custom_call_target="tpu_custom_call" | custom-call | tf_op jit(solution)/shard_map/moments/pallas_call | solution.py:565
  40.6 115.2 %solve.1 = (f32[1,128]{1,0:T(1,128)}, f32[1,128]{1,0:T(1,128)}) custom-call(f32[18,104,128]{2,1,0:T(8,128)} %get-tuple-element.12.refs_0_, f32[18,16,128]{2,1,0:T(8,128)} %get-tuple-element.13.refs_1_, f32[96,128]{1,0:T(8,128)} %get-tuple-element.14.refs_2_, f32[1,1,128]{2,1,0:T(1,128)} %get-tuple-element.22.affine.refs_3_, ...), custom_call_target="tpu_custom_call" | custom-call | tf_op jit(solution)/shard_map/solve/pallas_call | solution.py:589
  155.8 0.0 copy-start.2
  155.8 0.0 copy-start.3
  155.8 0.6 copy-done.2
  156.4 0.0 copy-done.3
  156.5 0.1 reshape_squeeze.7
  156.7 0.7 copy.17
  157.4 0.1 reshape_squeeze.6
  157.5 0.7 copy.16
  (11 shorter events, 0.1 us)
Async XLA Ops:
  1.3 0.7 copy-start.6
  1.3 0.7 copy-start.1
  2.1 0.7 copy-start.4
  2.1 0.7 copy-start.5
  3.1 0.7 copy-start
  155.8 0.6 copy-start.2
  155.8 0.7 copy-start.3
where the time goes:
time: 158 us
  Pallas kernels  149 us (94%)
  local copies, waits for them, and re-layouts  5.98 us (4%)
    pallas_call x1, Pallas kernels, on_device(): pl.pallas_call(functools.partial(solve_kernel, steps, ITERS // steps), ou...  115 us
    pallas_call x1, Pallas kernels, on_device(): pl.pallas_call(exchange_kernel, out_shape=(moved, moved, jax.ShapeDtypeSt...  24.4 us
    pallas_call x1, Pallas kernels, on_device(): pl.pallas_call(moments_kernel, out_shape=(jax.ShapeDtypeStruct((OTHERS +...  9.81 us
    unnamed x17, local copies, waits for them, and re-layouts  3.48 us

commit v1 on v0

--- a/solution.py
+++ b/solution.py
@@ -8,8 +8,7 @@
 from jax.sharding import PartitionSpec as P
 
 BLOCK = 256
-ITERS = 10
-STEP = 2
+FIRST, SECOND, AHEAD = 6, 4, 1
 SPACING = 0.5
 DAMPING = 1.0
 OFFSETS = (
@@ -44,7 +43,12 @@
 
 
 SELF = (0, 0, 0)
-REACH = (SELF, *sorted({s for o in OFFSETS for s in shifts(o)} - {SELF}))
+REACH = (
+    SELF,
+    *sorted(
+        {s for o in OFFSETS for s in shifts(o)} - {SELF}, key=lambda s: (-sum(map(abs, s)), s)
+    ),
+)
 OTHERS = len(REACH) - 1
 GREET = tuple(sorted({s for s in REACH[1:]} | {tuple(-p for p in s) for s in REACH[1:]}))
 
@@ -233,15 +237,53 @@
         shares[j, COMPS : COMPS + 1, :] = jnp.sum(total, axis=0, keepdims=True)
 
 
-def solve_kernel(steps, groups, *refs):
+def split(x):
+    big = x * 4097.0
+    high = big - (big - x)
+    return high, x - high
+
+
+def exact_product(x, y):
+    (xh, xl), (yh, yl) = split(x), split(y)
+    product = x * y
+    return product, ((xh * yh - product) + xh * yl + xl * yh) + xl * yl
+
+
+def lane_total(values, small, bound):
+    grid = bound * 256.0
+    top = (values + grid) - grid
+    rest = values - top
+    grid = grid * 2.0**-16
+    middle = (rest + grid) - grid
+    small = small + (rest - middle)
+    top, middle, small = (jnp.sum(v, axis=1, keepdims=True) for v in (top, middle, small))
+    high = top + middle
+    back = high - top
+    return high, ((top - (high - back)) + (middle - back)) + small
+
+
+def compensated(parts):
+    total, error = parts[0], jnp.zeros_like(parts[0])
+    for part in parts[1:]:
+        following = total + part
+        back = following - total
+        error = error + ((total - (following - back)) + (part - back))
+        total = following
+    high, low = total[0:1], error[0:1] + total[1:2]
+    both = high + low
+    return both, low - (both - high)
+
+
+def solve_kernel(plan, *refs):
+    first_steps, second_steps, ahead, amounts = plan
+    steps = len(amounts)
     blocks, shares, own, affine, affine_there, keep = refs[:6]
     update, residual = refs[6:8]
-    shares_there, matrix, inverse, plane, basis, lifted_basis = refs[8:14]
-    pair_sum, line_sum, pair_send, line_send = refs[14:18]
-    rest = refs[18:]
+    shares_there, matrix, inverse, chain, chain_lifted, basis, lifted = refs[8:15]
+    pair_sum, line_sum, pair_send, line_send = refs[15:19]
+    rest = refs[19:]
     send_rows, got_rows, back_rows, got_back = (rest[k * steps : (k + 1) * steps] for k in range(4))
     share_sent, share_got, halo_sems, sum_sems = rest[4 * steps :]
-    count = 2 * steps + 1
     first, second, third = (lax.axis_index(a) for a in AXES)
     size_first, size_second, size_third = (lax.axis_size(a) for a in AXES)
     in_pair = second * size_third + third
@@ -346,7 +388,7 @@
             total = total + inverse[group(a), :] * col[a]
         return jnp.sum(total, axis=0, keepdims=True)
 
-    def couple(step, vectors):
+    def couple(step, vectors, meanwhile=None):
         amount = len(vectors)
         cols = [column(v) for v in vectors]
         for r, v in enumerate(vectors):
@@ -380,6 +422,8 @@
                     halo_sems.at[step, 3],
                     device_at(REACH[j], 1),
                 ).start()
+        if meanwhile is not None:
+            meanwhile()
         sums = [[blocks[0, group(a), :] * v for a in range(COMPS)] for v in vectors]
         rows_there, back_there = got_rows[step], got_back[step]
         pltpu.make_async_copy(rows_there, rows_there, halo_sems.at[step, 1]).wait()
@@ -405,115 +449,157 @@
         pltpu.make_async_copy(back_there, back_there, halo_sems.at[step, 2]).wait()
         return results
 
-    def reduce_all(value, parity):
-        pair_send[parity] = value
-        pair_sum[parity, in_pair] = value
+    def pair_part(at):
+        return pair_sum.at[at, pl.ds(0, pair_size - 1)]
+
+    def line_part(at):
+        return line_sum.at[at, pl.ds(0, size_first - 1)]
+
+    def wait_for(part, sem):
+        pltpu.make_async_copy(part, part, sem).wait()
+
+    def start_sum(high, low, at):
+        for row, value in ((0, high), (1, low)):
+            pair_send[at, row : row + 1, :] = value
+            pair_sum[at, in_pair, row : row + 1, :] = value
 
         @pl.loop(1, pair_size)
         def _(k):
             remote(
-                pair_send.at[parity],
-                pair_sum.at[parity, in_pair],
-                sum_sems.at[parity, 0],
-                sum_sems.at[parity, 1],
+                pair_send.at[at],
+                pair_sum.at[at, in_pair],
+                sum_sems.at[at, 0],
+                sum_sems.at[at, 1],
                 pair_peer(k),
             ).start()
 
-        part = pair_sum.at[parity, pl.ds(0, pair_size - 1)]
-        pltpu.make_async_copy(part, part, sum_sems.at[parity, 1]).wait()
-        total = pair_sum[parity, 0]
-        for k in range(1, pair_size):
-            total = total + pair_sum[parity, k]
-        line_send[parity] = total
-        line_sum[parity, first] = total
+    def go_on_sum(at):
+        wait_for(pair_part(at), sum_sems.at[at, 1])
+        high, low = compensated([pair_sum[at, k] for k in range(pair_size)])
+        for row, value in ((0, high), (1, low)):
+            line_send[at, row : row + 1, :] = value
+            line_sum[at, first, row : row + 1, :] = value
 
         @pl.loop(1, size_first)
         def _(k):
             remote(
-                line_send.at[parity],
-                line_sum.at[parity, first],
-                sum_sems.at[parity, 2],
-                sum_sems.at[parity, 3],
+                line_send.at[at],
+                line_sum.at[at, first],
+                sum_sems.at[at, 2],
+                sum_sems.at[at, 3],
                 line_peer(k),
             ).start()
 
-        row_part = line_sum.at[parity, pl.ds(0, size_first - 1)]
-        pltpu.make_async_copy(row_part, row_part, sum_sems.at[parity, 3]).wait()
-        total = line_sum[parity, 0]
-        for k in range(1, size_first):
-            total = total + line_sum[parity, k]
-        pltpu.make_async_copy(part, part, sum_sems.at[parity, 0]).wait()
-        pltpu.make_async_copy(row_part, row_part, sum_sems.at[parity, 2]).wait()
-        return total
-
-    basis[...] = jnp.zeros_like(basis)
-    lifted_basis[...] = jnp.zeros_like(lifted_basis)
-    start, start_lifted = as_row(right), precondition(right)
-    for at in (0, steps + 1):
-        basis[at : at + 1, :] = start
-        lifted_basis[at : at + 1, :] = start_lifted
-    update[...] = jnp.zeros_like(update)
-
-    major = jnp.zeros((TILES, LANES), jnp.int32)
-    for k in range(1, count + 1):
-        major = major + jnp.where(lane >= k * count, 1, 0)
-    minor = lane - count * major
-
-    def form(mask):
-        return jnp.where(mask & (lane < count * count), 1.0, 0.0)
-
-    @pl.loop(0, groups)
-    def _(number):
-        for step in range(steps):
-            places = [step] + ([steps + 1 + step] if step < steps - 1 else [])
-            found = couple(step, [lifted_basis[at : at + 1, :] for at in places])
-            for at, col in zip(places, found):
-                basis[at + 1 : at + 2, :] = as_row(col)
-                lifted_basis[at + 1 : at + 2, :] = precondition(col)
-        gram = cross(basis[...], lifted_basis[...])
-        spread = jnp.zeros((16, LANES), F32)
-        for k in range(count):
-            moved = pltpu.roll(gram, k * count, 1) if k else gram
-            spread = spread + jnp.where(wide_sub == k, moved, 0.0)
-        mine = jnp.sum(spread, axis=0, keepdims=True)
-        g = jnp.broadcast_to(reduce_all(mine, lax.rem(number, 2)), (TILES, LANES))
-
-        def inner(x, y):
-            return jnp.sum(g * x * y, axis=1, keepdims=True)
-
-        p_major, p_minor = form(major == 0), form(minor == 0)
-        r_major, r_minor = form(major == steps + 1), form(minor == steps + 1)
+    def end_sum(at):
+        wait_for(line_part(at), sum_sems.at[at, 3])
+        high, low = compensated([line_sum[at, k] for k in range(size_first)])
+        wait_for(pair_part(at), sum_sems.at[at, 0])
+        wait_for(line_part(at), sum_sems.at[at, 2])
+        return tuple(jnp.broadcast_to(v, (TILES, LANES)) for v in (high, low))
+
+    def largest(values):
+        return jnp.max(jnp.abs(values), axis=1, keepdims=True)
+
+    def gram(count, ys, zs):
+        y_bound, z_bound = largest(ys), largest(zs)
+        row_of, lane_of = iotas(ys.shape[0])
+        high = low = jnp.zeros(ys.shape, F32)
+        for j in range(count):
+            at = (lane_of == row_of * count + j) & (row_of < count)
+            product, error = exact_product(ys, zs[j : j + 1, :])
+            h, l = lane_total(product, error, y_bound * z_bound[j : j + 1, :])
+            high, low = jnp.where(at, h, high), jnp.where(at, l, low)
+        return tuple(jnp.sum(v, axis=0, keepdims=True) for v in (high, low))
+
+    def iterate(count, amount, at_p, at_r, high, low):
+        major = jnp.zeros((TILES, LANES), jnp.int32)
+        for k in range(1, count + 1):
+            major = major + jnp.where(lane >= k * count, 1, 0)
+        minor = lane - count * major
+
+        def form(mask):
+            return jnp.where(mask & (lane < count * count), 1.0, 0.0)
+
+        g_bound = largest(high)
+
+        def inner(x, y, bound):
+            product, error = exact_product(x, y)
+            values, small = exact_product(product, high)
+            total = lane_total(values, small + (product * low + error * high), g_bound * bound)
+            return total[0] + total[1]
+
+        p_major, p_minor = form(major == at_p), form(minor == at_p)
+        r_major, r_minor = form(major == at_r), form(minor == at_r)
         u_minor = jnp.zeros((TILES, LANES), F32)
-        product = inner(r_major, r_minor)
-        for _ in range(steps):
+        p_most = r_most = jnp.ones((TILES, 1), F32)
+        product = inner(r_major, r_minor, r_most)
+        for _ in range(amount):
             a_major = p_major + pltpu.roll(p_major, count, 1)
             a_minor = p_minor + pltpu.roll(p_minor, 1, 1)
-            alpha = product / inner(p_major, a_minor)
+            a_most = 2.0 * p_most
+            alpha = product / inner(p_major, a_minor, p_most * a_most)
             u_minor = u_minor + alpha * p_minor
             r_major = r_major - alpha * a_major
             r_minor = r_minor - alpha * a_minor
-            following = inner(r_major, r_minor)
+            r_most = (r_most + jnp.abs(alpha) * a_most) * 1.01
+            following = inner(r_major, r_minor, r_most * r_most)
             ratio = following / product
             p_major = r_major + ratio * p_major
             p_minor = r_minor + ratio * p_minor
+            p_most = (r_most + jnp.abs(ratio) * p_most) * 1.01
             product = following
-
-        def combined(minor_form, vectors):
-            both = jnp.concatenate([minor_form, minor_form], axis=0)
-            weights = jnp.sum(
-                jnp.where((wide_lane == wide_sub) & (wide_lane < count), both, 0.0),
-                axis=1,
-                keepdims=True,
-            )
-            return jnp.sum(weights * vectors, axis=0, keepdims=True)
-
-        ys, zs = basis[...], lifted_basis[0:16, :]
-        update[...] += combined(u_minor, zs)
-        for at, shape in ((0, p_minor), (steps + 1, r_minor)):
-            basis[at : at + 1, :] = combined(shape, ys)
-            lifted_basis[at : at + 1, :] = combined(shape, zs)
-
-    residual[...] = basis[steps + 1 : steps + 2, :]
+        return u_minor, r_minor, p_minor
+
+    def combined(count, minor_form, vectors, by=0):
+        both = jnp.concatenate([minor_form, minor_form], axis=0)
+        weights = jnp.sum(
+            jnp.where((wide_lane + by == wide_sub) & (wide_lane < count), both, 0.0),
+            axis=1,
+            keepdims=True,
+        )
+        return jnp.sum(weights * vectors, axis=0, keepdims=True)
+
+    for ref in (chain, chain_lifted, basis, lifted):
+        ref[...] = jnp.zeros_like(ref)
+    chain[0:1, :] = as_row(right)
+    chain_lifted[0:1, :] = precondition(right)
+
+    def extend(step, places, ys, zs, meanwhile=None):
+        found = couple(step, [zs[at : at + 1, :] for at in places], meanwhile)
+        for at, col in zip(places, found):
+            ys[at + 1 : at + 2, :] = as_row(col)
+            zs[at + 1 : at + 2, :] = precondition(col)
+
+    for step in range(first_steps):
+        extend(step, [step], chain, chain_lifted)
+    count = first_steps + 1
+    start_sum(*gram(count, chain[0:8, :], chain_lifted[0:8, :]), 0)
+    for step in range(first_steps, first_steps + ahead):
+        extend(
+            step,
+            [step],
+            chain,
+            chain_lifted,
+            functools.partial(go_on_sum, 0) if step == first_steps else None,
+        )
+    u_form, r_form, p_form = iterate(count, first_steps, 0, 0, *end_sum(0))
+    ys, zs = chain[...], chain_lifted[...]
+    part = combined(count, u_form, zs)
+    at_r = second_steps + 1
+    for begin, shape in ((0, p_form), (at_r, r_form)):
+        for by in range(ahead + 1):
+            at = begin + by
+            basis[at : at + 1, :] = combined(count, shape, ys, by)
+            lifted[at : at + 1, :] = combined(count, shape, zs, by)
+    for step in range(first_steps + ahead, steps):
+        degree = step - first_steps
+        extend(step, [degree, at_r + degree][: amounts[step]], basis, lifted)
+    count = 2 * second_steps + 1
+    start_sum(*gram(count, basis[...], lifted[...]), 1)
+    go_on_sum(1)
+    u_form, r_form, _ = iterate(count, second_steps, 0, at_r, *end_sum(1))
+    update[...] = part + combined(count, u_form, lifted[...])
+    residual[...] = combined(count, r_form, basis[...])
 
 
 def vmem(*shape):
@@ -583,11 +669,12 @@
         name="moments",
     )(source_points, target_points, near, far, normals, weight, affine_row)
 
-    steps = STEP
-    amounts = [2] * (steps - 1) + [1]
+    later = SECOND - AHEAD
+    amounts = (1,) * (FIRST + AHEAD) + (2,) * (later - 1) + (1,)
+    steps = len(amounts)
     pair_size = sizes[1] * sizes[2]
     update, residual = pl.pallas_call(
-        functools.partial(solve_kernel, steps, ITERS // steps),
+        functools.partial(solve_kernel, (FIRST, SECOND, AHEAD, amounts)),
         out_shape=(jax.ShapeDtypeStruct((1, LANES), F32),) * 2,
         in_specs=[in_vmem] * 6,
         out_specs=[in_vmem] * 2,
@@ -595,13 +682,11 @@
             vmem(OTHERS, 16, LANES),
             vmem(COMPS, 16, LANES),
             vmem(ROWS, LANES),
-            vmem(16, LANES),
-            vmem(16, LANES),
-            vmem(LANES, LANES),
-            vmem(2, pair_size, 1, LANES),
-            vmem(2, sizes[0], 1, LANES),
-            vmem(2, 1, LANES),
-            vmem(2, 1, LANES),
+            *[vmem(16, LANES)] * 4,
+            vmem(2, pair_size, 2, LANES),
+            vmem(2, sizes[0], 2, LANES),
+            vmem(2, 2, LANES),
+            vmem(2, 2, LANES),
             *[vmem(1, r, LANES) for r in amounts],
             *[vmem(OTHERS, r, LANES) for r in amounts],
             *[vmem(OTHERS, r, LANES) for r in amounts],

time: 158 us -> 124 us (0.78)
  Pallas kernels: 149 us -> 115 us
    pallas_call x1, Pallas kernels: 115 us -> 80.9 us  [on_device(): pl.pallas_call(functools.partial(solve_kernel, (FIRST, SECOND, AHEAD, amo...]
where the time goes in v1:
time: 124 us
  Pallas kernels  115 us (93%)
  local copies, waits for them, and re-layouts  5.98 us (5%)
  other arithmetic  1.47 us (1%)
  between operations  1.43 us (1%)
    pallas_call x1, Pallas kernels, on_device(): pl.pallas_call(functools.partial(solve_kernel, (FIRST, SECOND, AHEAD, amo...  80.9 us
    pallas_call x1, Pallas kernels, on_device(): pl.pallas_call(exchange_kernel, out_shape=(moved, moved, jax.ShapeDtypeSt...  24.4 us
    pallas_call x1, Pallas kernels, on_device(): pl.pallas_call(moments_kernel, out_shape=(jax.ShapeDtypeStruct((OTHERS +...  9.81 us
    unnamed x17, local copies, waits for them, and re-layouts  3.48 us

profile of v1, /device:TPU:1, one launch (start us, length us, event | category | flops | bytes accessed | tf_op | source)
XLA Modules:
  0.0 124.0 jit_solution(8978359951354494420)
XLA Ops:
  1.3 0.0 copy-start.6
  1.3 0.0 copy-start.1
  1.4 0.6 copy-done.6
  2.0 0.1 reshape.192
  2.1 0.0 copy-done.1
  2.1 0.0 copy-start.4
  2.1 0.0 copy-start.5
  2.1 0.6 copy-done.4
  2.7 0.0 copy-done.5
  2.7 0.1 fusion.4
  2.8 0.1 copy.15
  2.9 0.1 add.127
  3.0 0.1 add.128
  3.1 0.0 copy-start
  3.1 0.1 tile.10
  3.2 0.6 pad_bitcast_fusion.refs_5_
  3.8 0.0 copy-done
  3.8 0.1 copy.14
  3.9 0.1 reshape.188
  4.0 0.6 fusion.9
  4.6 1.1 reshape.189
  5.7 0.8 fusion.weight
  6.5 24.4 %exchange.1 = (f32[3,13,4,2,512]{4,3,2,1,0:T(2,128)}, f32[3,13,4,2,512]{4,3,2,1,0:T(2,128)}, f32[17,1,128]{2,1,0:T(1,128)}) custom-call(f32[3,13,1,4,2,512]{5,4,3,2,1,0:T(2,128)} %target.3, f32[1,128]{1,0:T(1,128)} %get-tuple-element.23.affine), custom_call_target="tpu_custom_call" | custom-call | tf_op jit(solution)/shard_map/exchange/pallas_call | solution.py:639
  30.8 9.8 %moments.1 = (f32[18,104,128]{2,1,0:T(8,128)}, f32[18,16,128]{2,1,0:T(8,128)}, f32[96,128]{1,0:T(8,128)}) custom-call(f32[3,13,1,4,2,512]{5,4,3,2,1,0:T(2,128)} %source.1, f32[3,13,1,4,2,512]{5,4,3,2,1,0:T(2,128)} %target.3, f32[3,13,4,2,512]{4,3,2,1,0:T(2,128)} %get-tuple-element.10.near, f32[3,13,4,2,512]{4,3,2,1,0:T(2,128)} %get-tuple-element.11.far, ...), custom_call_target="tpu_custom_call" | custom-call | tf_op jit(solution)/shard_map/moments/pallas_call | solution.py:651
  40.6 80.9 %solve.1 = (f32[1,128]{1,0:T(1,128)}, f32[1,128]{1,0:T(1,128)}) custom-call(f32[18,104,128]{2,1,0:T(8,128)} %get-tuple-element.12.refs_0_, f32[18,16,128]{2,1,0:T(8,128)} %get-tuple-element.13.refs_1_, f32[96,128]{1,0:T(8,128)} %get-tuple-element.14.refs_2_, f32[1,1,128]{2,1,0:T(1,128)} %get-tuple-element.22.affine.refs_3_, ...), custom_call_target="tpu_custom_call" | custom-call | tf_op jit(solution)/shard_map/solve/pallas_call | solution.py:676
  121.6 0.0 copy-start.2
  121.6 0.0 copy-start.3
  121.6 0.6 copy-done.2
  122.2 0.0 copy-done.3
  122.3 0.1 reshape_squeeze.7
  122.4 0.7 copy.17
  123.1 0.1 reshape_squeeze.6
  123.2 0.7 copy.16
  (11 shorter events, 0.1 us)
Async XLA Ops:
  1.3 0.7 copy-start.6
  1.3 0.7 copy-start.1
  2.1 0.7 copy-start.4
  2.1 0.7 copy-start.5
  3.1 0.7 copy-start
  121.6 0.6 copy-start.2
  121.6 0.7 copy-start.3

commit v2 on v1

--- a/solution.py
+++ b/solution.py
@@ -53,23 +53,21 @@
 GREET = tuple(sorted({s for s in REACH[1:]} | {tuple(-p for p in s) for s in REACH[1:]}))
 
 
-def pieces():
-    found = []
-    for index, offset in enumerate(OFFSETS):
-        for shift in shifts(offset):
-            if shift == SELF:
-                continue
-            if offset[1] == 0:
-                low, count = 0, TY
-            elif shift[1] == 0:
-                low, count = (1 if offset[1] > 0 else 0), TY - 1
-            else:
-                low, count = (0 if offset[1] > 0 else TY - 1), 1
-            found.append((index, shift, low, count, 0 if shift[2] == 0 else 1))
-    return tuple(found)
-
-
-PIECES = pieces()
+def spans(part, shift, length):
+    if part == 0:
+        return 0, length
+    if shift == 0:
+        return (1 if part > 0 else 0), length - 1
+    return (0 if part > 0 else length - 1), 1
+
+
+ORDER = tuple(sorted(range(len(OFFSETS)), key=lambda d: ((0, 2, 1)[OFFSETS[d][0]], d)))
+PIECES = tuple(
+    (d, s, *spans(OFFSETS[d][1], s[1], TY), *spans(OFFSETS[d][2], s[2], TZ))
+    for d in ORDER
+    for s in shifts(OFFSETS[d])
+    if s != SELF
+)
 
 
 def device_at(shift, sign):
@@ -91,35 +89,6 @@
     )
 
 
-def exchange_kernel(target, affine, near, far, affine_there, sent, got):
-    barrier = pltpu.get_barrier_semaphore()
-    for shift in GREET:
-        pl.semaphore_signal(barrier, inc=1, device_id=device_at(shift, 1), device_id_type=MESH)
-    pl.semaphore_wait(barrier, len(GREET))
-    copies = []
-    for number, (index, shift, low, count, which) in enumerate(PIECES):
-        span = pl.ds(low, count)
-        place = (near, far)[which]
-        copies.append(
-            remote(
-                target.at[:, index, 0, span],
-                place.at[:, index, span],
-                sent.at[number],
-                got.at[number],
-                device_at(shift, -1),
-            )
-        )
-    for number, shift in enumerate(REACH[1:]):
-        at = len(PIECES) + number
-        copies.append(
-            remote(affine, affine_there.at[number], sent.at[at], got.at[at], device_at(shift, -1))
-        )
-    for copy in copies:
-        copy.start()
-    for copy in copies:
-        copy.wait()
-
-
 def iotas(rows=TILES):
     return (
         lax.broadcasted_iota(jnp.int32, (rows, LANES), 0),
@@ -139,102 +108,6 @@
         precision=lax.Precision.HIGHEST,
         preferred_element_type=F32,
     )
-
-
-def moments_kernel(
-    source,
-    target,
-    near,
-    far,
-    normal,
-    weight,
-    affine,
-    blocks,
-    shares,
-    own,
-    slab,
-    here,
-    here_weighted,
-    there,
-    there_weighted,
-    packed,
-):
-    sub, lane = iotas()
-    slot = lane & (TILES - 1)
-    blocks[...] = jnp.zeros_like(blocks)
-    shares[...] = jnp.zeros_like(shares)
-    own[...] = jnp.zeros_like(own)
-    packed[...] = jnp.zeros_like(packed)
-    here[WIDE:, :] = jnp.zeros((LANES - WIDE, here.shape[1]), F32)
-    there[ROWS:, :] = jnp.zeros((LANES - ROWS, there.shape[1]), F32)
-    same = sub == slot
-    for index, offset in enumerate(OFFSETS):
-        for y in range(TY):
-            for c in range(3):
-                slab[c, 2 * y : 2 * y + 2, :] = source[c, index, 0, y]
-                slab[3 + c, 2 * y : 2 * y + 2, :] = normal[c, index, 0, y]
-        for y in range(TY):
-            before = (y - offset[1]) % TY
-            shift_y = (y - offset[1]) // TY
-            for z in range(TZ):
-                back = (z - offset[2]) % TZ
-                shift_z = (z - offset[2]) // TZ
-                shift = (offset[0], -shift_y, -shift_z)
-                to, come = y * TZ + z, before * TZ + back
-                for c in range(3):
-                    slab[6 + c, to : to + 1, :] = normal[c, index, 0, before, back : back + 1, :]
-                    if shift == SELF:
-                        row = target[c, index, 0, y, z : z + 1, :]
-                    elif shift[2] == 0:
-                        row = near[c, index, y, z : z + 1, :]
-                    else:
-                        row = far[c, index, y, z : z + 1, :]
-                    slab[9 + c, to : to + 1, :] = row
-                slab[12, to : to + 1, :] = weight[index, come : come + 1, :]
-        share, share_there = weight[index], slab[12]
-        for c in range(3):
-            n, m = slab[3 + c], slab[6 + c]
-            for e in range(4):
-                at = (4 * c + e) * TILES
-                a = n * slab[e] if e < 3 else n
-                b = -(m * slab[9 + e]) if e < 3 else -m
-                here[at : at + TILES, :] = a
-                here_weighted[at : at + TILES, :] = a * share
-                there[at : at + TILES, :] = b
-                there_weighted[at : at + TILES, :] = b * share_there
-        along = sum(part * slab[3 + c] for c, part in enumerate(offset) if part != 0)
-        here[ROWS:WIDE, :] = along
-        here_weighted[ROWS:WIDE, :] = along * share
-        own[...] += cross(here_weighted[:ROWS, :], here[...])
-        pair = cross(here_weighted[...], there[...])
-        back = cross(there_weighted[...], there[...])
-        for a in range(COMPS):
-            at = a * TILES
-            packed[a : a + 1, :] = jnp.sum(
-                jnp.where(same, back[at : at + TILES, :], 0.0), axis=0, keepdims=True
-            )
-        second, third = sub // TZ + offset[1], sub % TZ + offset[2]
-        slot_y, slot_z = slot // TZ, slot % TZ
-        all_slots = packed[...]
-        for shift in shifts(offset):
-            j = REACH.index(shift)
-            meets = (slot_y + TY * shift[1] == second) & (slot_z + TZ * shift[2] == third)
-            blocks[j] += jnp.where(tiled(meets, WIDE // TILES), pair, 0.0)
-            owned = jnp.ones((TILES, LANES), jnp.bool_)
-            from_y, from_z = slot_y - offset[1] + TY * shift[1], slot_z - offset[2] + TZ * shift[2]
-            owned = (from_y >= 0) & (from_y < TY) & (from_z >= 0) & (from_z < TZ)
-            shares[j] += jnp.where(tiled(owned, 2), all_slots, 0.0)
-    own[...] = jnp.where(tiled(same, COMPS), own[...], 0.0)
-    row = affine[0]
-    columns = [
-        jnp.sum(jnp.where(lane == sub + a * TILES, row, 0.0), axis=1, keepdims=True)
-        for a in range(COMPS + 1)
-    ]
-    for j in range(OTHERS + 1):
-        total = jnp.zeros((TILES, LANES), F32)
-        for a in range(COMPS + 1):
-            total = total + blocks[j, a * TILES : (a + 1) * TILES, :] * columns[a]
-        shares[j, COMPS : COMPS + 1, :] = jnp.sum(total, axis=0, keepdims=True)
 
 
 def split(x):
@@ -274,16 +147,32 @@
     return both, low - (both - high)
 
 
-def solve_kernel(plan, *refs):
+def step_kernel(plan, *refs):
     first_steps, second_steps, ahead, amounts = plan
     steps = len(amounts)
-    blocks, shares, own, affine, affine_there, keep = refs[:6]
-    update, residual = refs[6:8]
-    shares_there, matrix, inverse, chain, chain_lifted, basis, lifted = refs[8:15]
-    pair_sum, line_sum, pair_send, line_send = refs[15:19]
-    rest = refs[19:]
+    source_out, target_out, normal_out, weight_out, counts, affines, anchor = refs[:7]
+    update, residual = refs[7:9]
+    source, target, normal, weight, moved, affine, affine_there = refs[9:16]
+    slab, here, here_weighted, there, there_weighted, packed, small = refs[16:23]
+    small_count, masked, blocks, shares, own = refs[23:28]
+    shares_there, matrix, inverse, chain, chain_lifted, basis, lifted = refs[28:35]
+    pair_sum, line_sum, pair_send, line_send = refs[35:39]
+    rest = refs[39:]
     send_rows, got_rows, back_rows, got_back = (rest[k * steps : (k + 1) * steps] for k in range(4))
-    share_sent, share_got, halo_sems, sum_sems = rest[4 * steps :]
+    loaded, sent, got, share_sent, share_got, halo_sems, sum_sems = rest[4 * steps :]
+    loads = [
+        pltpu.make_async_copy(outer, ref, loaded.at[number])
+        for number, (outer, ref) in enumerate(
+            (
+                (target_out, target),
+                (source_out, source),
+                (normal_out, normal),
+                (weight_out, weight),
+            )
+        )
+    ]
+    for load in loads:
+        load.start()
     first, second, third = (lax.axis_index(a) for a in AXES)
     size_first, size_second, size_third = (lax.axis_size(a) for a in AXES)
     in_pair = second * size_third + third
@@ -307,17 +196,6 @@
     @pl.loop(1, size_first)
     def _(k):
         pl.semaphore_signal(barrier, inc=1, device_id=line_peer(k), device_id_type=MESH)
-
-    pl.semaphore_wait(barrier, len(GREET) + pair_size - 1 + size_first - 1)
-
-    for number, shift in enumerate(REACH[1:]):
-        remote(
-            shares.at[number + 1],
-            shares_there.at[number],
-            share_sent,
-            share_got,
-            device_at(shift, 1),
-        ).start()
 
     sub, lane = iotas()
     slot = lane & (TILES - 1)
@@ -331,9 +209,147 @@
     def group(a):
         return slice(a * TILES, (a + 1) * TILES)
 
-    keep_row = keep[0]
-    keep_column = column(keep_row)
-    row = affine[0]
+    def positions(tile):
+        return (first, second * TY + tile // TZ, third * TZ + tile % TZ)
+
+    extents = (size_first, size_second * TY, size_third * TZ)
+
+    def kept(tile):
+        x, y, z = positions(tile)
+        return jnp.where((x * extents[1] + y) * extents[2] + z != anchor[0], 1.0, 0.0)
+
+    for y in range(TY):
+        small[2 * y : 2 * y + 2, 0:COMPS] = affines[0, y]
+    affine_columns = [
+        small[:, a : a + 1] + (1.0 if a % 5 == 0 else 0.0) for a in range(COMPS)
+    ]
+    row = jnp.zeros((TILES, LANES), F32)
+    for a in range(COMPS):
+        row = row + jnp.where(eyes[a], affine_columns[a], 0.0)
+    row = jnp.sum(row, axis=0, keepdims=True)
+    row = jnp.where((lane[:1] >= ROWS) & (lane[:1] < WIDE), -SPACING, row)
+    affine[...] = row
+
+    pl.semaphore_wait(barrier, len(GREET) + pair_size - 1 + size_first - 1)
+    loads[0].wait()
+    copies = {}
+    for number, (index, shift, low, count, low_z, count_z) in enumerate(PIECES):
+        at = (slice(None), index, pl.ds(low, count), pl.ds(low_z, count_z))
+        copy = remote(
+            target.at[(slice(None), index, 0, *at[2:])],
+            moved.at[at],
+            sent.at[number],
+            got.at[number],
+            device_at(shift, -1),
+        )
+        copy.start()
+        copies.setdefault(index, []).append(copy)
+    affine_copies = []
+    for number, shift in enumerate(REACH[1:]):
+        at = len(PIECES) + number
+        affine_copies.append(
+            remote(affine, affine_there.at[number], sent.at[at], got.at[at], device_at(shift, -1))
+        )
+        affine_copies[-1].start()
+
+    for ref in (blocks, shares, own, packed):
+        ref[...] = jnp.zeros_like(ref)
+    points = here.shape[1]
+    here[WIDE:, :] = jnp.zeros((LANES - WIDE, points), F32)
+    there[ROWS:, :] = jnp.zeros((LANES - ROWS, points), F32)
+    numbers = lax.broadcasted_iota(jnp.int32, (TILES, points), 1)
+    tile_column = sub[:, 0:1]
+    for load in loads[1:]:
+        load.wait()
+    for index in ORDER:
+        offset = OFFSETS[index]
+        for y in range(TY):
+            for c in range(3):
+                slab[c, 2 * y : 2 * y + 2, :] = source[c, index, 0, y]
+                slab[3 + c, 2 * y : 2 * y + 2, :] = normal[c, index, 0, y]
+            slab[6, 2 * y : 2 * y + 2, :] = weight[index, 0, y]
+            small_count[2 * y : 2 * y + 2, :] = counts[0, y, :, index : index + 1]
+        inside = functools.reduce(
+            jnp.logical_and,
+            [
+                (p + o >= 0) & (p + o < extent)
+                for p, o, extent in zip(positions(tile_column), offset, extents)
+            ],
+        )
+        limit = jnp.where(inside, BLOCK * small_count[...], 0)
+        share = jnp.where(numbers < limit, slab[6], 0.0)
+        masked[index] = share
+        for c in range(3):
+            n = slab[3 + c]
+            for e in range(4):
+                at = (4 * c + e) * TILES
+                a = n * slab[e] if e < 3 else n
+                here[at : at + TILES, :] = a
+                here_weighted[index, at : at + TILES, :] = a * share
+        along = sum(part * slab[3 + c] for c, part in enumerate(offset) if part != 0)
+        here[ROWS:WIDE, :] = along
+        here_weighted[index, ROWS:WIDE, :] = along * share
+        own[...] += cross(here_weighted[index, :ROWS, :], here[...])
+    own[...] = jnp.where(tiled(same, COMPS), own[...], 0.0)
+
+    for index in ORDER:
+        offset = OFFSETS[index]
+        for copy in copies.get(index, ()):
+            copy.wait()
+        for y in range(TY):
+            before = (y - offset[1]) % TY
+            shift_y = (y - offset[1]) // TY
+            for z in range(TZ):
+                back = (z - offset[2]) % TZ
+                shift_z = (z - offset[2]) // TZ
+                to, come = y * TZ + z, before * TZ + back
+                local = (offset[0], -shift_y, -shift_z) == SELF
+                for c in range(3):
+                    slab[6 + c, to : to + 1, :] = normal[c, index, 0, before, back : back + 1, :]
+                    if local:
+                        slab[9 + c, to : to + 1, :] = target[c, index, 0, y, z : z + 1, :]
+                    else:
+                        slab[9 + c, to : to + 1, :] = moved[c, index, y, z : z + 1, :]
+                slab[12, to : to + 1, :] = masked[index, come : come + 1, :]
+        share_there = slab[12]
+        for c in range(3):
+            m = slab[6 + c]
+            for e in range(4):
+                at = (4 * c + e) * TILES
+                b = -(m * slab[9 + e]) if e < 3 else -m
+                there[at : at + TILES, :] = b
+                there_weighted[at : at + TILES, :] = b * share_there
+        pair = cross(here_weighted[index], there[...])
+        back = cross(there_weighted[...], there[...])
+        for a in range(COMPS):
+            packed[a : a + 1, :] = jnp.sum(
+                jnp.where(same, back[group(a), :], 0.0), axis=0, keepdims=True
+            )
+        to_y, to_z = sub // TZ + offset[1], sub % TZ + offset[2]
+        slot_y, slot_z = slot // TZ, slot % TZ
+        all_slots = packed[...]
+        for shift in shifts(offset):
+            j = REACH.index(shift)
+            meets = (slot_y + TY * shift[1] == to_y) & (slot_z + TZ * shift[2] == to_z)
+            blocks[j] += jnp.where(tiled(meets, WIDE // TILES), pair, 0.0)
+            from_y, from_z = slot_y - offset[1] + TY * shift[1], slot_z - offset[2] + TZ * shift[2]
+            owned = (from_y >= 0) & (from_y < TY) & (from_z >= 0) & (from_z < TZ)
+            shares[j] += jnp.where(tiled(owned, 2), all_slots, 0.0)
+    extended = [*affine_columns, jnp.full((TILES, 1), -SPACING, F32)]
+    for j in (*range(1, OTHERS + 1), 0):
+        total = jnp.zeros((TILES, LANES), F32)
+        for a in range(COMPS + 1):
+            total = total + blocks[j, group(a), :] * extended[a]
+        shares[j, COMPS : COMPS + 1, :] = jnp.sum(total, axis=0, keepdims=True)
+        if j > 0:
+            remote(
+                shares.at[j], shares_there.at[j - 1], share_sent, share_got, device_at(REACH[j], 1)
+            ).start()
+    for copy in affine_copies:
+        copy.wait()
+
+    keep_row, keep_one = kept(slot[:1]), kept(tile_column)
+    keep_column = [keep_one] * COMPS
     sums = []
     for a in range(COMPS):
         total = own[group(a), :] * row + blocks[0, group(a), :] * row
@@ -598,8 +614,17 @@
     start_sum(*gram(count, basis[...], lifted[...]), 1)
     go_on_sum(1)
     u_form, r_form, _ = iterate(count, second_steps, 0, at_r, *end_sum(1))
-    update[...] = part + combined(count, u_form, lifted[...])
-    residual[...] = combined(count, r_form, basis[...])
+    results = (
+        (update, part + combined(count, u_form, lifted[...])),
+        (residual, combined(count, r_form, basis[...])),
+    )
+    for out, row in results:
+        spread = jnp.zeros((TILES, LANES), F32)
+        for a, col in enumerate(column(row)):
+            spread = jnp.where(lane == a, col, spread)
+        small[...] = spread
+        for y in range(TY):
+            out[0, y] = small[2 * y : 2 * y + 2, 0:COMPS]
 
 
 def vmem(*shape):
@@ -609,76 +634,42 @@
 def on_device(source_points, target_points, normals, weights, blocks, affines, anchor):
     points = source_points.shape[5]
     dirs = len(OFFSETS)
-    in_vmem = pl.BlockSpec(memory_space=pltpu.VMEM)
     sizes = [lax.axis_size(a) for a in AXES]
-
-    tile = jnp.arange(TILES, dtype=jnp.int32)
-    x = lax.axis_index("gx")
-    y = lax.axis_index("gy") * TY + tile // TZ
-    z = lax.axis_index("gz") * TZ + tile % TZ
-    spans = (sizes[0], sizes[1] * TY, sizes[2] * TZ)
-    keep = ((x * spans[1] + y) * spans[2] + z != anchor[0]).astype(F32)
-    keep_row = jnp.pad(jnp.tile(keep, COMPS), (0, LANES - ROWS)).reshape(1, 1, LANES)
-    identity = jnp.eye(3, 4, dtype=F32).reshape(COMPS, 1)
-    matrix = (affines.reshape(COMPS, TILES) + identity).reshape(-1)
-    affine_row = jnp.concatenate(
-        [matrix, jnp.full((TILES,), -SPACING, F32), jnp.zeros((LANES - WIDE,), F32)]
-    ).reshape(1, 1, LANES)
-    offsets = jnp.array(OFFSETS, jnp.int32).T[:, :, None]
-    there = [p + o for p, o in zip((x, y, z), offsets)]
-    inside = functools.reduce(
-        jnp.logical_and, [(p >= 0) & (p < span) for p, span in zip(there, spans)]
-    )
-    limit = jnp.where(inside, BLOCK * blocks.reshape(dirs, TILES), 0)
-    slots = jnp.arange(points, dtype=jnp.int32)
-    live = (slots < limit[..., None]).astype(F32)
-    weight = weights.reshape(dirs, TILES, points) * live
-
-    moved = jax.ShapeDtypeStruct((3, dirs, TY, TZ, points), F32)
-    copies = len(PIECES) + OTHERS
-    near, far, affine_there = pl.pallas_call(
-        exchange_kernel,
-        out_shape=(moved, moved, jax.ShapeDtypeStruct((OTHERS, 1, LANES), F32)),
-        in_specs=[in_vmem] * 2,
-        out_specs=[in_vmem] * 3,
-        scratch_shapes=[pltpu.SemaphoreType.DMA((copies,)), pltpu.SemaphoreType.DMA((copies,))],
-        compiler_params=pltpu.CompilerParams(
-            collective_id=0, has_side_effects=True, vmem_limit_bytes=60 * 2**20
-        ),
-        name="exchange",
-    )(target_points, affine_row[0])
-
-    pairs, shares, own = pl.pallas_call(
-        moments_kernel,
-        out_shape=(
-            jax.ShapeDtypeStruct((OTHERS + 1, WIDE, LANES), F32),
-            jax.ShapeDtypeStruct((OTHERS + 1, 16, LANES), F32),
-            jax.ShapeDtypeStruct((ROWS, LANES), F32),
-        ),
-        in_specs=[in_vmem] * 7,
-        out_specs=[in_vmem] * 3,
-        scratch_shapes=[
-            vmem(13, TILES, points),
-            vmem(LANES, points),
-            vmem(WIDE, points),
-            vmem(LANES, points),
-            vmem(ROWS, points),
-            vmem(16, LANES),
-        ],
-        compiler_params=pltpu.CompilerParams(vmem_limit_bytes=60 * 2**20),
-        name="moments",
-    )(source_points, target_points, near, far, normals, weight, affine_row)
-
     later = SECOND - AHEAD
     amounts = (1,) * (FIRST + AHEAD) + (2,) * (later - 1) + (1,)
     steps = len(amounts)
     pair_size = sizes[1] * sizes[2]
-    update, residual = pl.pallas_call(
-        functools.partial(solve_kernel, (FIRST, SECOND, AHEAD, amounts)),
-        out_shape=(jax.ShapeDtypeStruct((1, LANES), F32),) * 2,
-        in_specs=[in_vmem] * 6,
+    anywhere = pl.BlockSpec(memory_space=pl.ANY)
+    in_vmem = pl.BlockSpec(memory_space=pltpu.VMEM)
+    in_smem = pl.BlockSpec(memory_space=pltpu.SMEM)
+    copies = len(PIECES) + OTHERS
+    dma = pltpu.SemaphoreType.DMA
+    last = (1, 2, 3, 0)
+    outs = pl.pallas_call(
+        functools.partial(step_kernel, (FIRST, SECOND, AHEAD, amounts)),
+        out_shape=(jax.ShapeDtypeStruct((1, TY, TZ, COMPS), F32),) * 2,
+        in_specs=[anywhere] * 4 + [in_vmem] * 2 + [in_smem],
         out_specs=[in_vmem] * 2,
         scratch_shapes=[
+            vmem(*source_points.shape),
+            vmem(*target_points.shape),
+            vmem(*normals.shape),
+            vmem(*weights.shape),
+            vmem(3, dirs, TY, TZ, points),
+            vmem(1, LANES),
+            vmem(OTHERS, 1, LANES),
+            vmem(13, TILES, points),
+            vmem(LANES, points),
+            vmem(dirs, WIDE, points),
+            vmem(LANES, points),
+            vmem(ROWS, points),
+            vmem(16, LANES),
+            vmem(TILES, LANES),
+            pltpu.VMEM((TILES, 1), jnp.int32),
+            vmem(dirs, TILES, points),
+            vmem(OTHERS + 1, WIDE, LANES),
+            vmem(OTHERS + 1, 16, LANES),
+            vmem(ROWS, LANES),
             vmem(OTHERS, 16, LANES),
             vmem(COMPS, 16, LANES),
             vmem(ROWS, LANES),
@@ -691,18 +682,28 @@
             *[vmem(OTHERS, r, LANES) for r in amounts],
             *[vmem(OTHERS, r, LANES) for r in amounts],
             *[vmem(OTHERS, r, LANES) for r in amounts],
-            pltpu.SemaphoreType.DMA,
-            pltpu.SemaphoreType.DMA,
-            pltpu.SemaphoreType.DMA((steps, 4)),
-            pltpu.SemaphoreType.DMA((2, 4)),
+            dma((4,)),
+            dma((copies,)),
+            dma((copies,)),
+            dma,
+            dma,
+            dma((steps, 4)),
+            dma((2, 4)),
         ],
         compiler_params=pltpu.CompilerParams(
-            collective_id=1, has_side_effects=True, vmem_limit_bytes=60 * 2**20
+            collective_id=0, has_side_effects=True, vmem_limit_bytes=60 * 2**20
         ),
-        name="solve",
-    )(pairs, shares, own, affine_row, affine_there, keep_row)
-    shape = affines.shape
-    return update[0, :ROWS].reshape(shape), residual[0, :ROWS].reshape(shape)
+        name="step",
+    )(
+        source_points,
+        target_points,
+        normals,
+        weights,
+        jnp.transpose(blocks, last),
+        jnp.transpose(affines, last),
+        anchor,
+    )
+    return tuple(jnp.transpose(out, (3, 0, 1, 2)) for out in outs)
 
 
 def solution(mesh):

time: 124 us -> 102 us (0.82)
  Pallas kernels: 115 us -> 98.2 us
  local copies, waits for them, and re-layouts: 5.98 us -> 1.94 us
  other arithmetic: 1.47 us -> 0 us
    pallas_call x3 -> x1, Pallas kernels: 115 us -> 98.2 us  [on_device(): pl.pallas_call(functools.partial(step_kernel, (FIRST, SECOND, AHEAD, amou...]
    reshape x3 -> x0, local copies, waits for them, and re-layouts: 1.81 us -> none  [the longest x1 1.08 us: on_device(): weight = weights.reshape(dirs, TILES, points) * live]
    unnamed x17 -> x6, local copies, waits for them, and re-layouts: 3.48 us -> 1.94 us
where the time goes in v2:
time: 102 us; the launch traced here: 101 us
  Pallas kernels  98.2 us (96%)
  local copies, waits for them, and re-layouts  1.94 us (2%)
  between operations  1.3 us (1%)
    pallas_call x1, Pallas kernels, on_device(): pl.pallas_call(functools.partial(step_kernel, (FIRST, SECOND, AHEAD, amou...  98.2 us

profile of v2, /device:TPU:1, one launch (start us, length us, event | category | flops | bytes accessed | tf_op | source)
XLA Modules:
  0.0 101.4 jit_solution(2451847301431672582)
XLA Ops:
  1.3 98.2 %step.1 = (f32[1,4,2,12]{3,2,1,0:T(2,128)}, f32[1,4,2,12]{3,2,1,0:T(2,128)}) custom-call(f32[3,13,1,4,2,512]{5,4,3,2,1,0:T(2,128)} %refs_0_.1, f32[3,13,1,4,2,512]{5,4,3,2,1,0:T(2,128)} %refs_1_.1, f32[3,13,1,4,2,512]{5,4,3,2,1,0:T(2,128)} %refs_2_.1, f32[13,1,4,2,512]{4,3,2,1,0:T(2,128)} %refs_3_.1, s32[1,4,2,13]{3,2,1,0:T(2,128)} %bitcast.4, ...), custom_call_target="tpu_custom_call" | custom-call | tf_op jit(solution)/shard_map/step/pallas_call | solution.py:648
  99.4 0.0 copy-start.1
  99.5 0.7 copy-done.1
  100.1 0.0 copy-start
  100.1 0.6 copy.12
  100.7 0.1 copy-done
  100.8 0.6 copy.13
Async XLA Ops:
  99.4 0.7 copy-start.1
  100.1 0.7 copy-start

commit v3 on v2

--- a/solution.py
+++ b/solution.py
@@ -78,6 +78,20 @@
     return tuple(there)
 
 
+def exists(shift):
+    found = True
+    for axis, part in zip(AXES, shift):
+        if part > 0:
+            found = jnp.logical_and(lax.axis_index(axis) + part < lax.axis_size(axis), found)
+        elif part < 0:
+            found = jnp.logical_and(lax.axis_index(axis) + part >= 0, found)
+    return found
+
+
+def either(condition, then, otherwise):
+    lax.cond(condition, lambda: (then(), None)[1], lambda: (otherwise(), None)[1])
+
+
 def remote(source, target, sent, got, device):
     return pltpu.make_async_remote_copy(
         src_ref=source,
@@ -159,7 +173,8 @@
     pair_sum, line_sum, pair_send, line_send = refs[35:39]
     rest = refs[39:]
     send_rows, got_rows, back_rows, got_back = (rest[k * steps : (k + 1) * steps] for k in range(4))
-    loaded, sent, got, share_sent, share_got, halo_sems, sum_sems = rest[4 * steps :]
+    zero_one, zero_two, zero_share, spare_one, spare_two, spare_share = rest[4 * steps :][:6]
+    loaded, sent, got, share_sent, share_got, halo_sems, sum_sems = rest[4 * steps + 6 :]
     loads = [
         pltpu.make_async_copy(outer, ref, loaded.at[number])
         for number, (outer, ref) in enumerate(
@@ -186,8 +201,17 @@
         return (lax.rem(first + k, size_first), second, third)
 
     barrier = pltpu.get_barrier_semaphore()
+    for ref in (moved, affine_there, zero_one, zero_two, zero_share):
+        ref[...] = jnp.zeros_like(ref)
+    neighbours = 0
     for shift in GREET:
-        pl.semaphore_signal(barrier, inc=1, device_id=device_at(shift, 1), device_id_type=MESH)
+        near = exists(shift)
+        neighbours = neighbours + jnp.where(near, 1, 0)
+
+        @pl.when(near)
+        def _(shift=shift):
+            pl.semaphore_signal(barrier, inc=1, device_id=device_at(shift, 1), device_id_type=MESH)
+
 
     @pl.loop(1, pair_size)
     def _(k):
@@ -230,8 +254,17 @@
     row = jnp.where((lane[:1] >= ROWS) & (lane[:1] < WIDE), -SPACING, row)
     affine[...] = row
 
-    pl.semaphore_wait(barrier, len(GREET) + pair_size - 1 + size_first - 1)
+    pl.semaphore_wait(barrier, neighbours + (pair_size - 1 + size_first - 1))
     loads[0].wait()
+    zeros = {1: (zero_one, spare_one), 2: (zero_two, spare_two), 16: (zero_share, spare_share)}
+    ahead_there = [exists(shift) for shift in REACH[1:]]
+    behind_there = [exists(tuple(-part for part in shift)) for shift in REACH[1:]]
+
+    def fill(count, place, number, arrival, departure):
+        nothing, spare = zeros[count]
+        pltpu.make_async_copy(nothing, place, arrival).start()
+        pltpu.make_async_copy(nothing, spare.at[number], departure).start()
+
     copies = {}
     for number, (index, shift, low, count, low_z, count_z) in enumerate(PIECES):
         at = (slice(None), index, pl.ds(low, count), pl.ds(low_z, count_z))
@@ -242,15 +275,16 @@
             got.at[number],
             device_at(shift, -1),
         )
-        copy.start()
-        copies.setdefault(index, []).append(copy)
+        number = REACH.index(shift) - 1
+        pl.when(behind_there[number])(copy.start)
+        copies.setdefault(index, []).append((copy, number))
     affine_copies = []
     for number, shift in enumerate(REACH[1:]):
         at = len(PIECES) + number
         affine_copies.append(
             remote(affine, affine_there.at[number], sent.at[at], got.at[at], device_at(shift, -1))
         )
-        affine_copies[-1].start()
+        pl.when(behind_there[number])(affine_copies[-1].start)
 
     for ref in (blocks, shares, own, packed):
         ref[...] = jnp.zeros_like(ref)
@@ -294,8 +328,8 @@
 
     for index in ORDER:
         offset = OFFSETS[index]
-        for copy in copies.get(index, ()):
-            copy.wait()
+        for copy, number in copies.get(index, ()):
+            pl.when(ahead_there[number])(copy.wait_recv)
         for y in range(TY):
             before = (y - offset[1]) % TY
             shift_y = (y - offset[1]) // TY
@@ -336,17 +370,37 @@
             owned = (from_y >= 0) & (from_y < TY) & (from_z >= 0) & (from_z < TZ)
             shares[j] += jnp.where(tiled(owned, 2), all_slots, 0.0)
     extended = [*affine_columns, jnp.full((TILES, 1), -SPACING, F32)]
-    for j in (*range(1, OTHERS + 1), 0):
+    for j in range(OTHERS + 1):
         total = jnp.zeros((TILES, LANES), F32)
         for a in range(COMPS + 1):
             total = total + blocks[j, group(a), :] * extended[a]
         shares[j, COMPS : COMPS + 1, :] = jnp.sum(total, axis=0, keepdims=True)
-        if j > 0:
-            remote(
-                shares.at[j], shares_there.at[j - 1], share_sent, share_got, device_at(REACH[j], 1)
-            ).start()
-    for copy in affine_copies:
-        copy.wait()
+    for number, shift in enumerate(REACH[1:]):
+        copy = remote(
+            shares.at[number + 1],
+            shares_there.at[number],
+            share_sent,
+            share_got,
+            device_at(shift, 1),
+        )
+        pl.when(ahead_there[number])(copy.start)
+
+        @pl.when(jnp.logical_not(behind_there[number]))
+        def _(number=number):
+            nothing = zeros[16][0]
+            pltpu.make_async_copy(nothing, shares_there.at[number], share_got).start()
+
+        @pl.when(jnp.logical_not(ahead_there[number]))
+        def _(number=number):
+            nothing, spare = zeros[16]
+            pltpu.make_async_copy(nothing, spare.at[number], share_sent).start()
+
+    for index in ORDER:
+        for copy, number in copies.get(index, ()):
+            pl.when(behind_there[number])(copy.wait_send)
+    for number, copy in enumerate(affine_copies):
+        pl.when(ahead_there[number])(copy.wait_recv)
+        pl.when(behind_there[number])(copy.wait_send)
 
     keep_row, keep_one = kept(slot[:1]), kept(tile_column)
     keep_column = [keep_one] * COMPS
@@ -406,17 +460,26 @@
 
     def couple(step, vectors, meanwhile=None):
         amount = len(vectors)
-        cols = [column(v) for v in vectors]
         for r, v in enumerate(vectors):
             send_rows[step][0, r : r + 1, :] = v
         for number, shift in enumerate(REACH[1:]):
-            remote(
+            copy = remote(
                 send_rows[step].at[0],
                 got_rows[step].at[number],
                 halo_sems.at[step, 0],
                 halo_sems.at[step, 1],
                 device_at(shift, -1),
-            ).start()
+            )
+            empty = functools.partial(
+                fill,
+                amount,
+                got_back[step].at[number],
+                number,
+                halo_sems.at[step, 3],
+                halo_sems.at[step, 0],
+            )
+            either(behind_there[number], copy.start, empty)
+        cols = [column(v) for v in vectors]
         local = []
         for j in range(OTHERS + 1):
             totals = [jnp.zeros((TILES, LANES), F32) for _ in vectors]
@@ -430,14 +493,23 @@
                     local.append(total)
                 else:
                     back_rows[step][j - 1, r : r + 1, :] = total
-            if j > 0:
-                remote(
-                    back_rows[step].at[j - 1],
-                    got_back[step].at[j - 1],
-                    halo_sems.at[step, 2],
-                    halo_sems.at[step, 3],
-                    device_at(REACH[j], 1),
-                ).start()
+        for number, shift in enumerate(REACH[1:]):
+            copy = remote(
+                back_rows[step].at[number],
+                got_back[step].at[number],
+                halo_sems.at[step, 2],
+                halo_sems.at[step, 3],
+                device_at(shift, 1),
+            )
+            empty = functools.partial(
+                fill,
+                amount,
+                got_rows[step].at[number],
+                OTHERS + number,
+                halo_sems.at[step, 1],
+                halo_sems.at[step, 2],
+            )
+            either(ahead_there[number], copy.start, empty)
         if meanwhile is not None:
             meanwhile()
         sums = [[blocks[0, group(a), :] * v for a in range(COMPS)] for v in vectors]
@@ -682,6 +754,12 @@
             *[vmem(OTHERS, r, LANES) for r in amounts],
             *[vmem(OTHERS, r, LANES) for r in amounts],
             *[vmem(OTHERS, r, LANES) for r in amounts],
+            vmem(1, LANES),
+            vmem(2, LANES),
+            vmem(16, LANES),
+            vmem(2 * OTHERS, 1, LANES),
+            vmem(2 * OTHERS, 2, LANES),
+            vmem(OTHERS, 16, LANES),
             dma((4,)),
             dma((copies,)),
             dma((copies,)),

time: 102 us -> 94.9 us (0.930)
  Pallas kernels: 98.2 us -> 91.4 us
    pallas_call x1, Pallas kernels: 98.2 us -> 91.4 us  [on_device(): pl.pallas_call(functools.partial(step_kernel, (FIRST, SECOND, AHEAD, amou...]
where the time goes in v3:
time: 94.9 us; the launch traced here: 94.6 us
  Pallas kernels  91.4 us (96%)
  local copies, waits for them, and re-layouts  1.94 us (2%)
  between operations  1.3 us (1%)
    pallas_call x1, Pallas kernels, on_device(): pl.pallas_call(functools.partial(step_kernel, (FIRST, SECOND, AHEAD, amou...  91.4 us
    unnamed x6, local copies, waits for them, and re-layouts  1.94 us

profile of v3, /device:TPU:1, one launch (start us, length us, event | category | flops | bytes accessed | tf_op | source)
XLA Modules:
  0.0 94.6 jit_solution(7602595920359158152)
XLA Ops:
  1.3 91.4 %step.1 = (f32[1,4,2,12]{3,2,1,0:T(2,128)}, f32[1,4,2,12]{3,2,1,0:T(2,128)}) custom-call(f32[3,13,1,4,2,512]{5,4,3,2,1,0:T(2,128)} %refs_0_.1, f32[3,13,1,4,2,512]{5,4,3,2,1,0:T(2,128)} %refs_1_.1, f32[3,13,1,4,2,512]{5,4,3,2,1,0:T(2,128)} %refs_2_.1, f32[13,1,4,2,512]{4,3,2,1,0:T(2,128)} %refs_3_.1, s32[1,4,2,13]{3,2,1,0:T(2,128)} %bitcast.4, ...), custom_call_target="tpu_custom_call" | custom-call | tf_op jit(solution)/shard_map/step/pallas_call | solution.py:720
  92.7 0.0 copy-start.1
  92.7 0.7 copy-done.1
  93.4 0.0 copy-start
  93.4 0.6 copy.12
  93.9 0.1 copy-done
  94.0 0.6 copy.13
Async XLA Ops:
  92.7 0.7 copy-start.1
  93.4 0.7 copy-start

commit v4 on v3

--- a/solution.py
+++ b/solution.py
@@ -8,7 +8,7 @@
 from jax.sharding import PartitionSpec as P
 
 BLOCK = 256
-FIRST, SECOND, AHEAD = 6, 4, 1
+FIRST, SECOND, AHEAD = 5, 5, 2
 SPACING = 0.5
 DAMPING = 1.0
 OFFSETS = (
@@ -50,6 +50,8 @@
     ),
 )
 OTHERS = len(REACH) - 1
+PAIRS = tuple(dict.fromkeys((s[0], s[2]) for s in REACH))
+MEMBERS = tuple({s[1]: REACH.index(s) for s in REACH if (s[0], s[2]) == pair} for pair in PAIRS)
 GREET = tuple(sorted({s for s in REACH[1:]} | {tuple(-p for p in s) for s in REACH[1:]}))
 
 
@@ -362,19 +364,44 @@
         to_y, to_z = sub // TZ + offset[1], sub % TZ + offset[2]
         slot_y, slot_z = slot // TZ, slot % TZ
         all_slots = packed[...]
+        for k, (pair_x, pair_z) in enumerate(PAIRS):
+            ways = [w for w in shifts(offset) if (w[0], w[2]) == (pair_x, pair_z)]
+            if not ways:
+                continue
+            meets = functools.reduce(
+                jnp.logical_or, [slot_y + TY * w[1] == to_y for w in ways]
+            ) & (slot_z + TZ * pair_z == to_z)
+            blocks[k] += jnp.where(tiled(meets, WIDE // TILES), pair, 0.0)
         for shift in shifts(offset):
             j = REACH.index(shift)
-            meets = (slot_y + TY * shift[1] == to_y) & (slot_z + TZ * shift[2] == to_z)
-            blocks[j] += jnp.where(tiled(meets, WIDE // TILES), pair, 0.0)
             from_y, from_z = slot_y - offset[1] + TY * shift[1], slot_z - offset[2] + TZ * shift[2]
             owned = (from_y >= 0) & (from_y < TY) & (from_z >= 0) & (from_z < TZ)
             shares[j] += jnp.where(tiled(owned, 2), all_slots, 0.0)
+    crossing_up = (sub // TZ == TY - 1) & (slot // TZ == 0)
+    crossing_down = (sub // TZ == 0) & (slot // TZ == TY - 1)
+    staying = jnp.logical_not(crossing_up | crossing_down)
+    sides = {0: staying, 1: crossing_up, -1: crossing_down}
+
+    def mixed(k, row_of):
+        value = jnp.broadcast_to(row_of(MEMBERS[k][0]), (TILES, LANES))
+        for side in (1, -1):
+            if side in MEMBERS[k]:
+                value = jnp.where(sides[side], row_of(MEMBERS[k][side]), value)
+        return value
+
+    def parted(k, total):
+        return [
+            (j, jnp.sum(jnp.where(sides[side], total, 0.0), axis=0, keepdims=True))
+            for side, j in MEMBERS[k].items()
+        ]
+
     extended = [*affine_columns, jnp.full((TILES, 1), -SPACING, F32)]
-    for j in range(OTHERS + 1):
+    for k in range(len(PAIRS)):
         total = jnp.zeros((TILES, LANES), F32)
         for a in range(COMPS + 1):
-            total = total + blocks[j, group(a), :] * extended[a]
-        shares[j, COMPS : COMPS + 1, :] = jnp.sum(total, axis=0, keepdims=True)
+            total = total + blocks[k, group(a), :] * extended[a]
+        for j, part in parted(k, total):
+            shares[j, COMPS : COMPS + 1, :] = part
     for number, shift in enumerate(REACH[1:]):
         copy = remote(
             shares.at[number + 1],
@@ -404,11 +431,12 @@
 
     keep_row, keep_one = kept(slot[:1]), kept(tile_column)
     keep_column = [keep_one] * COMPS
+    mixes = [mixed(k, lambda j: affine_there[j - 1] if j else row) for k in range(len(PAIRS))]
     sums = []
     for a in range(COMPS):
-        total = own[group(a), :] * row + blocks[0, group(a), :] * row
-        for j in range(OTHERS):
-            total = total + blocks[j + 1, group(a), :] * affine_there[j]
+        total = own[group(a), :] * row
+        for k, mix in enumerate(mixes):
+            total = total + blocks[k, group(a), :] * mix
         sums.append(total)
     everything = pltpu.make_async_copy(shares_there, shares_there, share_got)
     everything.wait()
@@ -480,19 +508,19 @@
             )
             either(behind_there[number], copy.start, empty)
         cols = [column(v) for v in vectors]
-        local = []
-        for j in range(OTHERS + 1):
+        local = [None] * amount
+        for k in range(len(PAIRS)):
             totals = [jnp.zeros((TILES, LANES), F32) for _ in vectors]
             for a in range(COMPS):
-                block = blocks[j, group(a), :]
+                block = blocks[k, group(a), :]
                 for r in range(amount):
                     totals[r] = totals[r] + block * cols[r][a]
             for r in range(amount):
-                total = jnp.sum(totals[r], axis=0, keepdims=True)
-                if j == 0:
-                    local.append(total)
-                else:
-                    back_rows[step][j - 1, r : r + 1, :] = total
+                for j, part in parted(k, totals[r]):
+                    if j == 0:
+                        local[r] = part
+                    else:
+                        back_rows[step][j - 1, r : r + 1, :] = part
         for number, shift in enumerate(REACH[1:]):
             copy = remote(
                 back_rows[step].at[number],
@@ -512,14 +540,19 @@
             either(ahead_there[number], copy.start, empty)
         if meanwhile is not None:
             meanwhile()
-        sums = [[blocks[0, group(a), :] * v for a in range(COMPS)] for v in vectors]
         rows_there, back_there = got_rows[step], got_back[step]
         pltpu.make_async_copy(rows_there, rows_there, halo_sems.at[step, 1]).wait()
-        for j in range(OTHERS):
-            for r in range(amount):
-                v = rows_there[j, r : r + 1, :]
-                for a in range(COMPS):
-                    sums[r][a] = sums[r][a] + blocks[j + 1, group(a), :] * v
+        sums = [[None] * COMPS for _ in vectors]
+        for k in range(len(PAIRS)):
+            mixes = [
+                mixed(k, lambda j, r=r, v=v: rows_there[j - 1, r : r + 1, :] if j else v)
+                for r, v in enumerate(vectors)
+            ]
+            for a in range(COMPS):
+                block = blocks[k, group(a), :]
+                for r in range(amount):
+                    part = block * mixes[r]
+                    sums[r][a] = part if k == 0 else sums[r][a] + part
         pltpu.make_async_copy(back_there, back_there, halo_sems.at[step, 3]).wait()
         results = []
         for r in range(amount):
@@ -699,6 +732,17 @@
             out[0, y] = small[2 * y : 2 * y + 2, 0:COMPS]
 
 
+def finish_kernel(first, second, first_out, second_out, sems):
+    copies = [
+        pltpu.make_async_copy(first, first_out, sems.at[0]),
+        pltpu.make_async_copy(second, second_out, sems.at[1]),
+    ]
+    for copy in copies:
+        copy.start()
+    for copy in copies:
+        copy.wait()
+
+
 def vmem(*shape):
     return pltpu.VMEM(shape, F32)
 
@@ -739,7 +783,7 @@
             vmem(TILES, LANES),
             pltpu.VMEM((TILES, 1), jnp.int32),
             vmem(dirs, TILES, points),
-            vmem(OTHERS + 1, WIDE, LANES),
+            vmem(len(PAIRS), WIDE, LANES),
             vmem(OTHERS + 1, 16, LANES),
             vmem(ROWS, LANES),
             vmem(OTHERS, 16, LANES),
@@ -781,6 +825,14 @@
         jnp.transpose(affines, last),
         anchor,
     )
+    outs = pl.pallas_call(
+        finish_kernel,
+        out_shape=tuple(jax.ShapeDtypeStruct(out.shape, F32) for out in outs),
+        in_specs=[anywhere] * 2,
+        out_specs=[anywhere] * 2,
+        scratch_shapes=[dma((2,))],
+        name="finish",
+    )(*outs)
     return tuple(jnp.transpose(out, (3, 0, 1, 2)) for out in outs)
 
 

time: 94.9 us -> 91.2 us (0.961)
  local copies, waits for them, and re-layouts: 1.94 us -> 0 us
  Pallas kernels: 91.4 us -> 89.5 us
    pallas_call x1, Pallas kernels: 91.4 us -> 88.2 us  [on_device(): pl.pallas_call(functools.partial(step_kernel, (FIRST, SECOND, AHEAD, amou...]
    unnamed x6 -> x0, local copies, waits for them, and re-layouts: 1.94 us -> none
    pallas_call x0 -> x1, Pallas kernels: none -> 1.37 us  [on_device(): pl.pallas_call(finish_kernel, out_shape=tuple((jax.ShapeDtypeStruct(out.s...]
where the time goes in v4:
time: 91.2 us; the launch traced here: 91 us
  Pallas kernels  89.5 us (98%)
  between operations  1.45 us (2%)
    pallas_call x1, Pallas kernels, on_device(): pl.pallas_call(functools.partial(step_kernel, (FIRST, SECOND, AHEAD, amou...  88.2 us

profile of v4, /device:TPU:1, one launch (start us, length us, event | category | flops | bytes accessed | tf_op | source)
XLA Modules:
  0.0 91.0 jit_solution(6587517785020220852)
XLA Ops:
  1.3 88.2 %step.1 = (f32[1,4,2,12]{3,2,1,0:T(2,128)}, f32[1,4,2,12]{3,2,1,0:T(2,128)}) custom-call(f32[3,13,1,4,2,512]{5,4,3,2,1,0:T(2,128)} %refs_0_.1, f32[3,13,1,4,2,512]{5,4,3,2,1,0:T(2,128)} %refs_1_.1, f32[3,13,1,4,2,512]{5,4,3,2,1,0:T(2,128)} %refs_2_.1, f32[13,1,4,2,512]{4,3,2,1,0:T(2,128)} %refs_3_.1, s32[1,4,2,13]{3,2,1,0:T(2,128)} %bitcast.4, ...), custom_call_target="tpu_custom_call" | custom-call | tf_op jit(solution)/shard_map/step/pallas_call | solution.py:764
  89.5 1.4 %finish.1 = (f32[1,4,2,12]{3,2,1,0:T(2,128)}, f32[1,4,2,12]{3,2,1,0:T(2,128)}) custom-call(f32[1,4,2,12]{3,2,1,0:T(2,128)} %get-tuple-element.6.first, f32[1,4,2,12]{3,2,1,0:T(2,128)} %get-tuple-element.7.second), custom_call_target="tpu_custom_call" | custom-call | tf_op jit(solution)/shard_map/finish/pallas_call | solution.py:828

commit v5 on v4

--- a/solution.py
+++ b/solution.py
@@ -126,6 +126,24 @@
     )
 
 
+def halves(x):
+    top = x.astype(jnp.bfloat16)
+    return top, (x - top.astype(F32)).astype(jnp.bfloat16)
+
+
+def narrow_cross(left, right):
+    return lax.dot_general(
+        left, right, (((1,), (1,)), ((), ())), preferred_element_type=F32
+    )
+
+
+def cross_of(left_top, left_rest, right):
+    top, rest = halves(right)
+    both = narrow_cross(jnp.concatenate([left_top, left_rest], axis=0), top)
+    count = left_top.shape[0]
+    return both[:count] + (both[count:] + narrow_cross(left_top, rest))
+
+
 def split(x):
     big = x * 4097.0
     high = big - (big - x)
@@ -169,11 +187,11 @@
     source_out, target_out, normal_out, weight_out, counts, affines, anchor = refs[:7]
     update, residual = refs[7:9]
     source, target, normal, weight, moved, affine, affine_there = refs[9:16]
-    slab, here, here_weighted, there, there_weighted, packed, small = refs[16:23]
-    small_count, masked, blocks, shares, own = refs[23:28]
-    shares_there, matrix, inverse, chain, chain_lifted, basis, lifted = refs[28:35]
-    pair_sum, line_sum, pair_send, line_send = refs[35:39]
-    rest = refs[39:]
+    slab, here, here_weighted, there, packed, small = refs[16:22]
+    small_count, masked, blocks, shares, own = refs[22:27]
+    shares_there, matrix, inverse, chain, chain_lifted, basis, lifted = refs[27:34]
+    pair_sum, line_sum, pair_send, line_send = refs[34:38]
+    rest = refs[38:]
     send_rows, got_rows, back_rows, got_back = (rest[k * steps : (k + 1) * steps] for k in range(4))
     zero_one, zero_two, zero_share, spare_one, spare_two, spare_share = rest[4 * steps :][:6]
     loaded, sent, got, share_sent, share_got, halo_sems, sum_sems = rest[4 * steps + 6 :]
@@ -293,6 +311,8 @@
     points = here.shape[1]
     here[WIDE:, :] = jnp.zeros((LANES - WIDE, points), F32)
     there[ROWS:, :] = jnp.zeros((LANES - ROWS, points), F32)
+    for index in ORDER:
+        here_weighted[index, WIDE + ROWS :, :] = jnp.zeros((TILES, points), F32)
     numbers = lax.broadcasted_iota(jnp.int32, (TILES, points), 1)
     tile_column = sub[:, 0:1]
     for load in loads[1:]:
@@ -325,7 +345,7 @@
         along = sum(part * slab[3 + c] for c, part in enumerate(offset) if part != 0)
         here[ROWS:WIDE, :] = along
         here_weighted[index, ROWS:WIDE, :] = along * share
-        own[...] += cross(here_weighted[index, :ROWS, :], here[...])
+        own[...] += cross_of(*halves(here_weighted[index, :ROWS, :]), here[...])
     own[...] = jnp.where(tiled(same, COMPS), own[...], 0.0)
 
     for index in ORDER:
@@ -354,9 +374,9 @@
                 at = (4 * c + e) * TILES
                 b = -(m * slab[9 + e]) if e < 3 else -m
                 there[at : at + TILES, :] = b
-                there_weighted[at : at + TILES, :] = b * share_there
-        pair = cross(here_weighted[index], there[...])
-        back = cross(there_weighted[...], there[...])
+                here_weighted[index, WIDE + at : WIDE + at + TILES, :] = b * share_there
+        both = cross_of(*halves(here_weighted[index]), there[...])
+        pair, back = both[:WIDE], both[WIDE : WIDE + ROWS]
         for a in range(COMPS):
             packed[a : a + 1, :] = jnp.sum(
                 jnp.where(same, back[group(a), :], 0.0), axis=0, keepdims=True
@@ -776,9 +796,8 @@
             vmem(OTHERS, 1, LANES),
             vmem(13, TILES, points),
             vmem(LANES, points),
-            vmem(dirs, WIDE, points),
+            vmem(dirs, WIDE + ROWS + TILES, points),
             vmem(LANES, points),
-            vmem(ROWS, points),
             vmem(16, LANES),
             vmem(TILES, LANES),
             pltpu.VMEM((TILES, 1), jnp.int32),

time: 91.2 us -> 85.3 us (0.935)
  Pallas kernels: 89.5 us -> 83.9 us
    pallas_call x1, Pallas kernels: 88.2 us -> 82.5 us  [on_device(): pl.pallas_call(functools.partial(step_kernel, (FIRST, SECOND, AHEAD, amou...]
where the time goes in v5:
time: 85.3 us; the launch traced here: 85.2 us
  Pallas kernels  83.9 us (98%)
  between operations  1.29 us (2%)
    pallas_call x1, Pallas kernels, on_device(): pl.pallas_call(functools.partial(step_kernel, (FIRST, SECOND, AHEAD, amou...  82.5 us

profile of v5, /device:TPU:1, one launch (start us, length us, event | category | flops | bytes accessed | tf_op | source)
XLA Modules:
  0.0 85.2 jit_solution(13797276664806898549)
XLA Ops:
  1.3 82.5 %step.1 = (f32[1,4,2,12]{3,2,1,0:T(2,128)}, f32[1,4,2,12]{3,2,1,0:T(2,128)}) custom-call(f32[3,13,1,4,2,512]{5,4,3,2,1,0:T(2,128)} %refs_0_.1, f32[3,13,1,4,2,512]{5,4,3,2,1,0:T(2,128)} %refs_1_.1, f32[3,13,1,4,2,512]{5,4,3,2,1,0:T(2,128)} %refs_2_.1, f32[13,1,4,2,512]{4,3,2,1,0:T(2,128)} %refs_3_.1, s32[1,4,2,13]{3,2,1,0:T(2,128)} %bitcast.4, ...), custom_call_target="tpu_custom_call" | custom-call | tf_op jit(solution)/shard_map/step/pallas_call | solution.py:784
  83.8 1.4 %finish.1 = (f32[1,4,2,12]{3,2,1,0:T(2,128)}, f32[1,4,2,12]{3,2,1,0:T(2,128)}) custom-call(f32[1,4,2,12]{3,2,1,0:T(2,128)} %get-tuple-element.6.first, f32[1,4,2,12]{3,2,1,0:T(2,128)} %get-tuple-element.7.second), custom_call_target="tpu_custom_call" | custom-call | tf_op jit(solution)/shard_map/finish/pallas_call | solution.py:847

commit v6 on v5

--- a/solution.py
+++ b/solution.py
@@ -50,6 +50,7 @@
     ),
 )
 OTHERS = len(REACH) - 1
+EARLY = 6
 PAIRS = tuple(dict.fromkeys((s[0], s[2]) for s in REACH))
 MEMBERS = tuple({s[1]: REACH.index(s) for s in REACH if (s[0], s[2]) == pair} for pair in PAIRS)
 GREET = tuple(sorted({s for s in REACH[1:]} | {tuple(-p for p in s) for s in REACH[1:]}))
@@ -274,38 +275,6 @@
     row = jnp.where((lane[:1] >= ROWS) & (lane[:1] < WIDE), -SPACING, row)
     affine[...] = row
 
-    pl.semaphore_wait(barrier, neighbours + (pair_size - 1 + size_first - 1))
-    loads[0].wait()
-    zeros = {1: (zero_one, spare_one), 2: (zero_two, spare_two), 16: (zero_share, spare_share)}
-    ahead_there = [exists(shift) for shift in REACH[1:]]
-    behind_there = [exists(tuple(-part for part in shift)) for shift in REACH[1:]]
-
-    def fill(count, place, number, arrival, departure):
-        nothing, spare = zeros[count]
-        pltpu.make_async_copy(nothing, place, arrival).start()
-        pltpu.make_async_copy(nothing, spare.at[number], departure).start()
-
-    copies = {}
-    for number, (index, shift, low, count, low_z, count_z) in enumerate(PIECES):
-        at = (slice(None), index, pl.ds(low, count), pl.ds(low_z, count_z))
-        copy = remote(
-            target.at[(slice(None), index, 0, *at[2:])],
-            moved.at[at],
-            sent.at[number],
-            got.at[number],
-            device_at(shift, -1),
-        )
-        number = REACH.index(shift) - 1
-        pl.when(behind_there[number])(copy.start)
-        copies.setdefault(index, []).append((copy, number))
-    affine_copies = []
-    for number, shift in enumerate(REACH[1:]):
-        at = len(PIECES) + number
-        affine_copies.append(
-            remote(affine, affine_there.at[number], sent.at[at], got.at[at], device_at(shift, -1))
-        )
-        pl.when(behind_there[number])(affine_copies[-1].start)
-
     for ref in (blocks, shares, own, packed):
         ref[...] = jnp.zeros_like(ref)
     points = here.shape[1]
@@ -317,7 +286,7 @@
     tile_column = sub[:, 0:1]
     for load in loads[1:]:
         load.wait()
-    for index in ORDER:
+    def source_part(index):
         offset = OFFSETS[index]
         for y in range(TY):
             for c in range(3):
@@ -346,6 +315,44 @@
         here[ROWS:WIDE, :] = along
         here_weighted[index, ROWS:WIDE, :] = along * share
         own[...] += cross_of(*halves(here_weighted[index, :ROWS, :]), here[...])
+
+    for index in ORDER[:EARLY]:
+        source_part(index)
+
+    pl.semaphore_wait(barrier, neighbours + (pair_size - 1 + size_first - 1))
+    loads[0].wait()
+    zeros = {1: (zero_one, spare_one), 2: (zero_two, spare_two), 16: (zero_share, spare_share)}
+    ahead_there = [exists(shift) for shift in REACH[1:]]
+    behind_there = [exists(tuple(-part for part in shift)) for shift in REACH[1:]]
+
+    def fill(count, place, number, arrival, departure):
+        nothing, spare = zeros[count]
+        pltpu.make_async_copy(nothing, place, arrival).start()
+        pltpu.make_async_copy(nothing, spare.at[number], departure).start()
+
+    copies = {}
+    for number, (index, shift, low, count, low_z, count_z) in enumerate(PIECES):
+        at = (slice(None), index, pl.ds(low, count), pl.ds(low_z, count_z))
+        copy = remote(
+            target.at[(slice(None), index, 0, *at[2:])],
+            moved.at[at],
+            sent.at[number],
+            got.at[number],
+            device_at(shift, -1),
+        )
+        number = REACH.index(shift) - 1
+        pl.when(behind_there[number])(copy.start)
+        copies.setdefault(index, []).append((copy, number))
+    affine_copies = []
+    for number, shift in enumerate(REACH[1:]):
+        at = len(PIECES) + number
+        affine_copies.append(
+            remote(affine, affine_there.at[number], sent.at[at], got.at[at], device_at(shift, -1))
+        )
+        pl.when(behind_there[number])(affine_copies[-1].start)
+
+    for index in ORDER[EARLY:]:
+        source_part(index)
     own[...] = jnp.where(tiled(same, COMPS), own[...], 0.0)
 
     for index in ORDER:
@@ -604,8 +611,7 @@
             pair_send[at, row : row + 1, :] = value
             pair_sum[at, in_pair, row : row + 1, :] = value
 
-        @pl.loop(1, pair_size)
-        def _(k):
+        for k in range(1, pair_size):
             remote(
                 pair_send.at[at],
                 pair_sum.at[at, in_pair],
@@ -621,8 +627,7 @@
             line_send[at, row : row + 1, :] = value
             line_sum[at, first, row : row + 1, :] = value
 
-        @pl.loop(1, size_first)
-        def _(k):
+        for k in range(1, size_first):
             remote(
                 line_send.at[at],
                 line_sum.at[at, first],

time: 85.3 us -> 84.9 us (level)
  no operation moved by 1% of the time
where the time goes in v6:
time: 84.9 us; the launch traced here: 84.7 us
  Pallas kernels  83.5 us (98%)
  between operations  1.29 us (2%)
    pallas_call x1, Pallas kernels, on_device(): pl.pallas_call(functools.partial(step_kernel, (FIRST, SECOND, AHEAD, amou...  82.1 us

profile of v6, /device:TPU:1, one launch (start us, length us, event | category | flops | bytes accessed | tf_op | source)
XLA Modules:
  0.0 84.7 jit_solution(1085072220981582125)
XLA Ops:
  1.3 82.1 %step.1 = (f32[1,4,2,12]{3,2,1,0:T(2,128)}, f32[1,4,2,12]{3,2,1,0:T(2,128)}) custom-call(f32[3,13,1,4,2,512]{5,4,3,2,1,0:T(2,128)} %refs_0_.1, f32[3,13,1,4,2,512]{5,4,3,2,1,0:T(2,128)} %refs_1_.1, f32[3,13,1,4,2,512]{5,4,3,2,1,0:T(2,128)} %refs_2_.1, f32[13,1,4,2,512]{4,3,2,1,0:T(2,128)} %refs_3_.1, s32[1,4,2,13]{3,2,1,0:T(2,128)} %bitcast.4, ...), custom_call_target="tpu_custom_call" | custom-call | tf_op jit(solution)/shard_map/step/pallas_call | solution.py:789
  83.4 1.4 %finish.1 = (f32[1,4,2,12]{3,2,1,0:T(2,128)}, f32[1,4,2,12]{3,2,1,0:T(2,128)}) custom-call(f32[1,4,2,12]{3,2,1,0:T(2,128)} %get-tuple-element.6.first, f32[1,4,2,12]{3,2,1,0:T(2,128)} %get-tuple-element.7.second), custom_call_target="tpu_custom_call" | custom-call | tf_op jit(solution)/shard_map/finish/pallas_call | solution.py:852

commit v7 on v6

--- a/solution.py
+++ b/solution.py
@@ -657,7 +657,7 @@
             high, low = jnp.where(at, h, high), jnp.where(at, l, low)
         return tuple(jnp.sum(v, axis=0, keepdims=True) for v in (high, low))
 
-    def iterate(count, amount, at_p, at_r, high, low):
+    def iterate(count, amount, at_p, at_r, high, low, final=False):
         major = jnp.zeros((TILES, LANES), jnp.int32)
         for k in range(1, count + 1):
             major = major + jnp.where(lane >= k * count, 1, 0)
@@ -679,7 +679,7 @@
         u_minor = jnp.zeros((TILES, LANES), F32)
         p_most = r_most = jnp.ones((TILES, 1), F32)
         product = inner(r_major, r_minor, r_most)
-        for _ in range(amount):
+        for number in range(amount):
             a_major = p_major + pltpu.roll(p_major, count, 1)
             a_minor = p_minor + pltpu.roll(p_minor, 1, 1)
             a_most = 2.0 * p_most
@@ -688,6 +688,8 @@
             r_major = r_major - alpha * a_major
             r_minor = r_minor - alpha * a_minor
             r_most = (r_most + jnp.abs(alpha) * a_most) * 1.01
+            if final and number == amount - 1:
+                break
             following = inner(r_major, r_minor, r_most * r_most)
             ratio = following / product
             p_major = r_major + ratio * p_major
@@ -743,7 +745,7 @@
     count = 2 * second_steps + 1
     start_sum(*gram(count, basis[...], lifted[...]), 1)
     go_on_sum(1)
-    u_form, r_form, _ = iterate(count, second_steps, 0, at_r, *end_sum(1))
+    u_form, r_form, _ = iterate(count, second_steps, 0, at_r, *end_sum(1), final=True)
     results = (
         (update, part + combined(count, u_form, lifted[...])),
         (residual, combined(count, r_form, basis[...])),

time: 84.9 us -> 84.9 us (level)
  no operation moved by 1% of the time
where the time goes in v7:
time: 84.9 us; the launch traced here: 84.7 us
  Pallas kernels  83.5 us (98%)
  between operations  1.29 us (2%)
    pallas_call x1, Pallas kernels, on_device(): pl.pallas_call(functools.partial(step_kernel, (FIRST, SECOND, AHEAD, amou...  82.1 us

profile of v7, /device:TPU:1, one launch (start us, length us, event | category | flops | bytes accessed | tf_op | source)
XLA Modules:
  0.0 84.7 jit_solution(1085072220981582125)
XLA Ops:
  1.3 82.1 %step.1 = (f32[1,4,2,12]{3,2,1,0:T(2,128)}, f32[1,4,2,12]{3,2,1,0:T(2,128)}) custom-call(f32[3,13,1,4,2,512]{5,4,3,2,1,0:T(2,128)} %refs_0_.1, f32[3,13,1,4,2,512]{5,4,3,2,1,0:T(2,128)} %refs_1_.1, f32[3,13,1,4,2,512]{5,4,3,2,1,0:T(2,128)} %refs_2_.1, f32[13,1,4,2,512]{4,3,2,1,0:T(2,128)} %refs_3_.1, s32[1,4,2,13]{3,2,1,0:T(2,128)} %bitcast.4, ...), custom_call_target="tpu_custom_call" | custom-call | tf_op jit(solution)/shard_map/step/pallas_call | solution.py:791
  83.4 1.4 %finish.1 = (f32[1,4,2,12]{3,2,1,0:T(2,128)}, f32[1,4,2,12]{3,2,1,0:T(2,128)}) custom-call(f32[1,4,2,12]{3,2,1,0:T(2,128)} %get-tuple-element.6.first, f32[1,4,2,12]{3,2,1,0:T(2,128)} %get-tuple-element.7.second), custom_call_target="tpu_custom_call" | custom-call | tf_op jit(solution)/shard_map/finish/pallas_call | solution.py:854
